TPU v7x, 768 devices: a whole 4x8x12 slice. The times are simulated.
768 devices in a mesh: grp: 24 (over z_hi, y), shard: 32 (over x, z_lo, core).
Axes of the slice: x: 4, y: 8, z: 12 (z_hi: 3, z_lo: 4; z = z_hi * 4 + z_lo), core: 2. Of those that a mesh axis runs over, the one named last changes fastest.
Arguments:
- bottom_out: bfloat16 [98304, 128], P(('grp', 'shard')), may hold values from -6 to 6
- lookups: int32 [98304, 1, 4], P(('grp', 'shard')), may hold values from 0 to 251903, as said below
- starts: int32 [24, 768], replicated, may hold values from 0 to 327
- tables: float32 [1, 251904, 128], P(None, 'shard'), may hold values from -0.3 to 0.3
- top_dense: bfloat16 [128, 1024], replicated, may hold values from -0.5 to 0.5
- top_pairs: float32 [1, 1024], replicated, may hold values from -6 to 6
- cotangent: float32 [98304, 1024], P(('grp', 'shard')), may hold values from -1.5 to 1.5
Outputs:
- activation: bfloat16 [98304, 1024], P(('grp', 'shard'))
- bottom_grad: float32 [98304, 128], P(('grp', 'shard'))
- table_grad: float32 [1, 32, 7872, 128], P(None, 'shard', 'grp')
Inputs may be any that keep to these rules, and one draw needn't show every extreme that they name: lookups % 328 is below 64, and 63 occurs.
All inputs are finite; a program needn't handle non-finite values.
Results may differ from a plain program's by a relative error of at most 0.0023.
Values sent between devices are 32-bit elements; how exact they have to be, the bound alone decides.
A program may use at most 32 MiB of HBM per device.

v0:
```python
import math

import jax
import jax.numpy as jnp
from jax import lax
from jax.sharding import PartitionSpec as P

HOT = 64


def sent_to_all(value, axis):
    size = lax.axis_size(axis)
    return lax.all_to_all(
        jnp.broadcast_to(value[None], (size, *value.shape)), axis, 0, 0, tiled=True
    )


def joined_along(blocks, dim):
    lengths = list(blocks.shape[1:])
    lengths[dim] *= blocks.shape[0]
    return jnp.moveaxis(blocks, 0, dim).reshape(lengths)


def gathered_copies(value, axis, dim):
    blocks = sent_to_all(value, axis)
    return joined_along(blocks, dim)


def cut_along(value, dim, size):
    before, after = (value.shape[:dim], value.shape[dim + 1 :])
    return jnp.moveaxis(value.reshape(*before, size, -1, *after), dim, 0)


def sum_at_owner(value, axis, dim):
    blocks = cut_along(value, dim, lax.axis_size(axis))
    arrived = lax.all_to_all(blocks, axis, split_axis=0, concat_axis=0, tiled=True)
    return arrived.sum(axis=0)


def pair_list(number):
    return [(former, latter) for former in range(number) for latter in range(former + 1, number)]


def pool_lookups(tables, picked, offset):
    rows_count = picked.shape[0]
    table_count = picked.shape[1]
    bag_count = picked.shape[2]
    rows_block = math.gcd(rows_count, 512)
    bag_block = math.gcd(bag_count, 8)
    bag_turns = bag_count // bag_block
    span_rows = tables.shape[1]
    table_ids = jnp.arange(table_count, dtype=jnp.int32)[None, :, None]

    def pool_step(turn, running):
        row_turn = turn // bag_turns
        bag_turn = turn % bag_turns
        chosen = lax.dynamic_slice(
            picked,
            (row_turn * rows_block, 0, bag_turn * bag_block),
            (rows_block, table_count, bag_block),
        )
        local = chosen - offset
        inside = (local >= 0) & (local < span_rows)
        fetched = tables[table_ids, jnp.clip(local, 0, span_rows - 1)]
        summed = jnp.sum(jnp.where(inside[..., None], fetched, 0.0), axis=2)
        current = lax.dynamic_slice_in_dim(running, row_turn * rows_block, rows_block, 0)
        return lax.dynamic_update_slice_in_dim(running, current + summed, row_turn * rows_block, 0)

    start_value = jnp.zeros((rows_count, table_count, tables.shape[2]), jnp.float32)
    return lax.fori_loop(0, rows_count // rows_block * bag_turns, pool_step, start_value)


def add_lookups(running_grad, grads, picked, offset, span_rows):
    rows_count = picked.shape[0]
    table_count = picked.shape[1]
    bag_count = picked.shape[2]
    rows_block = math.gcd(rows_count, 512)
    bag_block = math.gcd(bag_count, 8)
    bag_turns = bag_count // bag_block
    table_ids = jnp.arange(table_count, dtype=jnp.int32)[None, :, None]

    def add_step(turn, running):
        row_turn = turn // bag_turns
        bag_turn = turn % bag_turns
        chosen = lax.dynamic_slice(
            picked,
            (row_turn * rows_block, 0, bag_turn * bag_block),
            (rows_block, table_count, bag_block),
        )
        grads_block = lax.dynamic_slice_in_dim(grads, row_turn * rows_block, rows_block, 0)
        local = chosen - offset
        inside = (local >= 0) & (local < span_rows)
        updates = jnp.where(inside[..., None], grads_block[:, :, None, :], 0.0)
        return running.at[table_ids, jnp.clip(local, 0, span_rows - 1)].add(updates)

    return lax.fori_loop(0, rows_count // rows_block * bag_turns, add_step, running_grad)


def on_device(bottom_out, lookups, starts, tables, top_dense, top_pairs, cotangent):
    shard_pos = lax.axis_index("shard")
    grp_pos = lax.axis_index("grp")
    group_count = lax.axis_size("grp")
    span_rows = tables.shape[1]
    table_count = tables.shape[0]
    width = tables.shape[2]
    win_size = span_rows // group_count
    offset = shard_pos * span_rows
    my_starts = lax.dynamic_index_in_dim(starts, grp_pos, 0, keepdims=False)
    window = lookups // win_size
    inner = lookups % win_size
    own_rows = window * win_size + (inner + my_starts[window]) % win_size
    group_idx = gathered_copies(own_rows, "shard", 0)
    picked = group_idx
    pooled = sum_at_owner(pool_lookups(tables, picked, offset), "shard", 0)
    vectors = [bottom_out.astype(jnp.float32)] + [pooled[:, 0]]
    couples = pair_list(table_count + 1)
    pair_dots = jnp.stack(
        [jnp.sum(vectors[former] * vectors[latter], axis=-1) for former, latter in couples], axis=1
    )
    preact = jnp.dot(bottom_out, top_dense, preferred_element_type=jnp.float32)
    preact = preact + jnp.dot(pair_dots, top_pairs, precision=lax.Precision.HIGHEST)
    sigmoid_pre = jax.nn.sigmoid(preact)
    activation = (preact * sigmoid_pre).astype(jnp.bfloat16)
    pre_grad = cotangent * sigmoid_pre * (1.0 + preact * (1.0 - sigmoid_pre))
    pair_grad = jnp.dot(pre_grad, top_pairs.T, precision=lax.Precision.HIGHEST)
    vec_grads = [jnp.zeros_like(vector) for vector in vectors]
    for place, (former, latter) in enumerate(couples):
        vec_grads[former] = pair_grad * vectors[latter]
        vec_grads[latter] = pair_grad * vectors[former]
    pre_half = pre_grad.astype(jnp.bfloat16)
    bottom_grad = (
        lax.dot_general(
            pre_half, top_dense, (((1,), (1,)), ((), ())), preferred_element_type=jnp.float32
        )
        + vec_grads[0]
    )
    pooled_grad = jnp.stack(vec_grads[1:], axis=1)
    start_grad = jnp.zeros((table_count, span_rows, width), jnp.float32)
    picked = group_idx
    local_grad = add_lookups(
        start_grad, gathered_copies(pooled_grad, "shard", 0), picked, offset, span_rows
    )
    hot_range = jnp.arange(HOT, dtype=jnp.int32)
    owner_range = jnp.arange(group_count, dtype=jnp.int32)
    send_starts = lax.dynamic_slice_in_dim(my_starts, shard_pos * group_count, group_count, 0)
    send_index = (
        owner_range[:, None] * win_size + (send_starts[:, None] + hot_range[None, :]) % win_size
    )
    packed = local_grad[:, send_index]
    received = lax.all_to_all(packed, "grp", split_axis=1, concat_axis=1, tiled=True)
    recv_starts = lax.dynamic_slice_in_dim(starts, shard_pos * group_count + grp_pos, 1, 1)[:, 0]
    places = ((recv_starts[:, None] + hot_range[None, :]) % win_size).reshape(-1)
    flat_rows = received.reshape(table_count, group_count * HOT, width)
    table_grad = jnp.zeros((table_count, win_size, width), jnp.float32).at[:, places].add(flat_rows)
    return (activation, bottom_grad, table_grad[:, None])


def solution(mesh):
    in_specs = (
        P(("grp", "shard"), None),
        P(("grp", "shard"), None, None),
        P(),
        P(None, "shard", None),
        P(),
        P(),
        P(("grp", "shard"), None),
    )
    out_specs = (
        P(("grp", "shard"), None),
        P(("grp", "shard"), None),
        P(None, "shard", "grp", None),
    )
    return jax.shard_map(
        on_device, mesh=mesh, in_specs=in_specs, out_specs=out_specs, check_vma=False
    )
```

profile of v0, /device:TPU:1, one launch (start us, length us, event | category | flops | bytes accessed | tf_op | source)
XLA Modules:
  0.0 1075.6 jit_solution(1918025001826048108)
XLA Ops:
  5.6 14.0 %all-to-all-start = ((s32[32,128,1,4]{1,3,2,0:T(4,128)}), s32[32,128,1,4]{1,3,2,0:T(4,128)S(1)}, u32[]{:S(2)}, u32[]{:S(2)}) async-start(s32[32,128,1,4]{1,3,2,0:T(4,128)} %broadcast_in_dim.126), calls=%async_computation | async-start | bytes 131072 | tf_op jit(solution)/shard_map/all_to_all | solution.py:13
  28.6 683.7 %while.30 = (s32[]{:T(128)}, f32[4096,1,128]{2,1,0:T(1,128)S(1)}, s32[4096,1,4]{0,2,1:T(4,128)S(1)}, s32[]{:T(128)}, f32[1,7872,128]{2,1,0:T(8,128)}, /*index=5*/s32[]{:T(128)}, s32[]{:T(128)}, s32[]{:T(128)}, s32[]{:T(128)}) while((s32[]{:T(128)}, f32[4096,1,128]{2,1,0:T(1,128)S(1)}, s32[4096,1,4]{0,2,1:T(4,128)S(1)}, s32[]{:T(128)}, ...), condition=%wide.region_2.3_spmd, body=%wide.region_0.2_spmd.sunk | while | flops 552966 | bytes 4325543 | solution.py:70
  29.0 81.6 %gather_fusion = f32[2048,128]{1,0:T(8,128)S(1)} fusion(f32[1,7872,128]{2,1,0:T(8,128)} %get-tuple-element.409, s32[2048]{0:T(1024)S(1)} %reshape.302), kind=kCustom, calls=%fused_computation.clone.1 | custom fusion | bytes 2113536 | tf_op jit(solution)/shard_map/while/body/eval_jaxpr/gather | solution.py:64
  114.5 81.5 %gather_fusion = f32[2048,128]{1,0:T(8,128)S(1)} fusion(f32[1,7872,128]{2,1,0:T(8,128)} %get-tuple-element.409, s32[2048]{0:T(1024)S(1)} %reshape.302), kind=kCustom, calls=%fused_computation.clone.1 | custom fusion | bytes 2113536 | tf_op jit(solution)/shard_map/while/body/eval_jaxpr/gather | solution.py:64
  199.8 82.3 %gather_fusion = f32[2048,128]{1,0:T(8,128)S(1)} fusion(f32[1,7872,128]{2,1,0:T(8,128)} %get-tuple-element.409, s32[2048]{0:T(1024)S(1)} %reshape.302), kind=kCustom, calls=%fused_computation.clone.1 | custom fusion | bytes 2113536 | tf_op jit(solution)/shard_map/while/body/eval_jaxpr/gather | solution.py:64
  285.9 81.4 %gather_fusion = f32[2048,128]{1,0:T(8,128)S(1)} fusion(f32[1,7872,128]{2,1,0:T(8,128)} %get-tuple-element.409, s32[2048]{0:T(1024)S(1)} %reshape.302), kind=kCustom, calls=%fused_computation.clone.1 | custom fusion | bytes 2113536 | tf_op jit(solution)/shard_map/while/body/eval_jaxpr/gather | solution.py:64
  371.2 81.8 %gather_fusion = f32[2048,128]{1,0:T(8,128)S(1)} fusion(f32[1,7872,128]{2,1,0:T(8,128)} %get-tuple-element.409, s32[2048]{0:T(1024)S(1)} %reshape.302), kind=kCustom, calls=%fused_computation.clone.1 | custom fusion | bytes 2113536 | tf_op jit(solution)/shard_map/while/body/eval_jaxpr/gather | solution.py:64
  456.8 81.5 %gather_fusion = f32[2048,128]{1,0:T(8,128)S(1)} fusion(f32[1,7872,128]{2,1,0:T(8,128)} %get-tuple-element.409, s32[2048]{0:T(1024)S(1)} %reshape.302), kind=kCustom, calls=%fused_computation.clone.1 | custom fusion | bytes 2113536 | tf_op jit(solution)/shard_map/while/body/eval_jaxpr/gather | solution.py:64
  542.1 81.5 %gather_fusion = f32[2048,128]{1,0:T(8,128)S(1)} fusion(f32[1,7872,128]{2,1,0:T(8,128)} %get-tuple-element.409, s32[2048]{0:T(1024)S(1)} %reshape.302), kind=kCustom, calls=%fused_computation.clone.1 | custom fusion | bytes 2113536 | tf_op jit(solution)/shard_map/while/body/eval_jaxpr/gather | solution.py:64
  627.5 81.4 %gather_fusion = f32[2048,128]{1,0:T(8,128)S(1)} fusion(f32[1,7872,128]{2,1,0:T(8,128)} %get-tuple-element.409, s32[2048]{0:T(1024)S(1)} %reshape.302), kind=kCustom, calls=%fused_computation.clone.1 | custom fusion | bytes 2113536 | tf_op jit(solution)/shard_map/while/body/eval_jaxpr/gather | solution.py:64
  712.3 73.5 %all_to_all.20 = f32[32,128,1,128]{3,1,2,0:T(8,128)} all-to-all(f32[32,128,1,128]{3,1,2,0:T(8,128)S(1)} %bitcast.74), channel_id=1, replica_groups=mesh['grp'=24,'shard'=32] {'shard'}, dimensions={0} | all-to-all | bytes 4194304 | tf_op jit(solution)/shard_map/all_to_all | solution.py:36
  796.7 49.0 %all-to-all-done.2 = f32[32,128,1,128]{3,1,2,0:T(8,128)} async-done(((f32[32,128,1,128]{3,1,2,0:T(8,128)}), f32[32,128,1,128]{3,1,2,0:T(8,128)}, u32[]{:S(2)}, u32[]{:S(2)}) %all-to-all-start.2) | async-done | bytes 2097184 | tf_op jit(solution)/shard_map/all_to_all | solution.py:13
  847.9 174.6 %while.31 = (s32[]{:T(128)}, f32[1,7872,128]{2,1,0:T(8,128)}, s32[4096,1,4]{0,2,1:T(4,128)S(1)}, s32[]{:T(128)}, f32[4096,1,128]{2,0,1:T(8,128)}, /*index=5*/s32...) while((s32[]{:T(128)}, f32[1,7872,128]{2,1,0:T(8,128)}, ...), condition=%wide.region_7.8_spmd, body=%wide.region_5.7_spmd.sunk | while | flops 565254 | bytes 5099719 | solution.py:96
  851.9 17.8 %scatter_fusion = f32[7872,128]{1,0:T(8,128)} fusion(f32[7872,128]{1,0:T(8,128)} %bitcast.68, s32[2048]{0:T(1024)S(1)} %reshape.305, f32[2048,128]{1,0:T(8,128)S(1)} %bitcast.72), kind=kCustom, calls=%fused_computation.3.clone.1 | custom fusion | flops 262144 | bytes 3153920 | tf_op jit(solution)/shard_map/while
  873.7 17.8 %scatter_fusion = f32[7872,128]{1,0:T(8,128)} fusion(f32[7872,128]{1,0:T(8,128)} %bitcast.68, s32[2048]{0:T(1024)S(1)} %reshape.305, f32[2048,128]{1,0:T(8,128)S(1)} %bitcast.72), kind=kCustom, calls=%fused_computation.3.clone.1 | custom fusion | flops 262144 | bytes 3153920 | tf_op jit(solution)/shard_map/while
  895.5 17.9 %scatter_fusion = f32[7872,128]{1,0:T(8,128)} fusion(f32[7872,128]{1,0:T(8,128)} %bitcast.68, s32[2048]{0:T(1024)S(1)} %reshape.305, f32[2048,128]{1,0:T(8,128)S(1)} %bitcast.72), kind=kCustom, calls=%fused_computation.3.clone.1 | custom fusion | flops 262144 | bytes 3153920 | tf_op jit(solution)/shard_map/while
  917.4 17.8 %scatter_fusion = f32[7872,128]{1,0:T(8,128)} fusion(f32[7872,128]{1,0:T(8,128)} %bitcast.68, s32[2048]{0:T(1024)S(1)} %reshape.305, f32[2048,128]{1,0:T(8,128)S(1)} %bitcast.72), kind=kCustom, calls=%fused_computation.3.clone.1 | custom fusion | flops 262144 | bytes 3153920 | tf_op jit(solution)/shard_map/while
  939.2 17.9 %scatter_fusion = f32[7872,128]{1,0:T(8,128)} fusion(f32[7872,128]{1,0:T(8,128)} %bitcast.68, s32[2048]{0:T(1024)S(1)} %reshape.305, f32[2048,128]{1,0:T(8,128)S(1)} %bitcast.72), kind=kCustom, calls=%fused_computation.3.clone.1 | custom fusion | flops 262144 | bytes 3153920 | tf_op jit(solution)/shard_map/while
  961.1 17.8 %scatter_fusion = f32[7872,128]{1,0:T(8,128)} fusion(f32[7872,128]{1,0:T(8,128)} %bitcast.68, s32[2048]{0:T(1024)S(1)} %reshape.305, f32[2048,128]{1,0:T(8,128)S(1)} %bitcast.72), kind=kCustom, calls=%fused_computation.3.clone.1 | custom fusion | flops 262144 | bytes 3153920 | tf_op jit(solution)/shard_map/while
  982.9 17.8 %scatter_fusion = f32[7872,128]{1,0:T(8,128)} fusion(f32[7872,128]{1,0:T(8,128)} %bitcast.68, s32[2048]{0:T(1024)S(1)} %reshape.305, f32[2048,128]{1,0:T(8,128)S(1)} %bitcast.72), kind=kCustom, calls=%fused_computation.3.clone.1 | custom fusion | flops 262144 | bytes 3153920 | tf_op jit(solution)/shard_map/while
  1004.7 17.8 %scatter_fusion = f32[7872,128]{1,0:T(8,128)} fusion(f32[7872,128]{1,0:T(8,128)} %bitcast.68, s32[2048]{0:T(1024)S(1)} %reshape.305, f32[2048,128]{1,0:T(8,128)S(1)} %bitcast.72), kind=kCustom, calls=%fused_computation.3.clone.1 | custom fusion | flops 262144 | bytes 3153920 | tf_op jit(solution)/shard_map/while
  1028.3 14.0 %all-to-all-start.3 = ((f32[1,24,64,128]{3,2,0,1:T(8,128)}), f32[1,24,64,128]{3,2,0,1:T(8,128)S(1)}, u32[]{:S(2)}, u32[]{:S(2)}) async-start(f32[1,24,64,128]{3,2,0,1:T(8,128)} %bitcast.21), calls=%async_computation.3 | async-start | bytes 1572864 | tf_op jit(solution)/shard_map/all_to_all | solution.py:150
  1044.3 21.9 %all-to-all-done.3 = f32[1,24,64,128]{3,2,0,1:T(8,128)S(1)} async-done(((f32[1,24,64,128]{3,2,0,1:T(8,128)}), f32[1,24,64,128]{3,2,0,1:T(8,128)S(1)}, u32[]{:S(2)}, u32[]{:S(2)}) %all-to-all-start.3) | async-done | bytes 786464 | tf_op jit(solution)/shard_map/all_to_all | solution.py:150
  1066.2 9.4 scatter_custom_fusion.1
  (199 shorter events, 96.4 us)
Async XLA Ops:
  0.6 787.2 %copy-start = (bf16[128,1024]{1,0:T(8,128)(2,1)S(1)}, bf16[128,1024]{1,0:T(8,128)(2,1)}, u32[]{:S(2)}) copy-start(bf16[128,1024]{1,0:T(8,128)(2,1)} %param.15) | copy-start | bytes 786436
  2.4 2.5 copy-start.4
  5.6 21.9 %all-to-all-start = ((s32[32,128,1,4]{1,3,2,0:T(4,128)}), s32[32,128,1,4]{1,3,2,0:T(4,128)S(1)}, u32[]{:S(2)}, u32[]{:S(2)}) async-start(s32[32,128,1,4]{1,3,2,0:T(4,128)} %broadcast_in_dim.126), calls=%async_computation | async-start | bytes 131072 | tf_op jit(solution)/shard_map/all_to_all | solution.py:13
  785.9 1.8 copy-start.1
  785.9 1.9 copy-start.5
  785.9 1.9 copy-start.6
  791.1 54.6 %all-to-all-start.2 = ((f32[32,128,1,128]{3,1,2,0:T(8,128)}), f32[32,128,1,128]{3,1,2,0:T(8,128)}, u32[]{:S(2)}, u32[]{:S(2)}) async-start(f32[32,128,1,128]{3,1,2,0:T(8,128)} %broadcast_in_dim.129), calls=%async_computation.2 | async-start | bytes 4194304 | tf_op jit(solution)/shard_map/all_to_all | solution.py:13
  795.7 52.2 %copy-start.2 = (s32[2]{0:T(128)S(1)}, s32[2]{0:T(128)}, u32[]{:S(2)}) copy-start(s32[2]{0:T(128)} %constant.368) | copy-start | bytes 28
  795.7 52.2 %copy-start.3 = (s32[2]{0:T(128)S(1)}, s32[2]{0:T(128)}, u32[]{:S(2)}) copy-start(s32[2]{0:T(128)} %constant.367) | copy-start | bytes 28
  1028.3 37.9 %all-to-all-start.3 = ((f32[1,24,64,128]{3,2,0,1:T(8,128)}), f32[1,24,64,128]{3,2,0,1:T(8,128)S(1)}, u32[]{:S(2)}, u32[]{:S(2)}) async-start(f32[1,24,64,128]{3,2,0,1:T(8,128)} %bitcast.21), calls=%async_computation.3 | async-start | bytes 1572864 | tf_op jit(solution)/shard_map/all_to_all | solution.py:150
where the time goes:
time: 1080 us
  local copies, waits for them, and re-layouts  685 us (63%)
  other arithmetic  201 us (19%)
  waiting for transfers between devices  78.8 us (7%)
  blocking collectives  73.5 us (7%)
  starting transfers between devices  32.6 us (3%)
    gather x8, local copies, waits for them, and re-layouts, pool_step(): fetched = tables[table_ids, jnp.clip(local, 0, span_rows - 1)]  653 us
    while x32, other arithmetic  144 us
    all_to_all x1, blocking collectives, sum_at_owner(): lax.all_to_all(blocks, axis, split_axis=0, concat_axis=0, tiled=True)  73.5 us
    all_to_all x2, waiting for transfers between devices, sent_to_all(): lax.all_to_all(jnp.broadcast_to(value[None], (size, *value.shape)), axis,...  56.9 us
    reduce_sum x8, other arithmetic, pool_step(): summed = jnp.sum(jnp.where(inside[..., None], fetched, 0.0), axis=2)  23.4 us
    all_to_all x1, waiting for transfers between devices, on_device(): lax.all_to_all(packed, 'grp', split_axis=1, concat_axis=1, tiled=True)  21.9 us
  transfers between devices with their start and end apart: 3, of which 3 were waited for; matrix products, arithmetic and copies ran while one was open for 0% of the time, Pallas kernels for 0%

commit v1 on v0

v1 whole, which is shorter than its diff:
```python
import jax
import jax.numpy as jnp
from jax import lax
from jax.experimental import pallas as pl
from jax.experimental.pallas import tpu as pltpu
from jax.sharding import PartitionSpec as P

HOT = 64
WIN = 328
NX, NZ, NC = 4, 4, 2
ZH, NY = 3, 8
CHIPS = NX * NZ
GROUPS = ZH * NY
B = 128
D = 128
OWN = GROUPS * HOT
ROWS = NC * OWN
PAD = WIN + HOT
OUT_ROWS = 336
F32, BF16, I32 = jnp.float32, jnp.bfloat16, jnp.int32
MESH = pl.DeviceIdType.MESH


def split_bf16(value):
    high = value.astype(BF16)
    return high, (value - high.astype(F32)).astype(BF16)


def kernel(
    starts_ref, idx_ref, places_ref, v0_ref, dense_ref, pairs_ref, cot_ref, tables_ref,
    act_ref, bgrad_ref, tgrad_ref,
    win, hot, hot_t, idxs, et, part, rx, qz, zr, vs, pgs, grads, pre_dense, lsend, lrecv, outb, grecv, place_hot,
    local_sem, hot_sem, idx_send, idx_recv, vz_send, vz_recv, vx_send, vx_recv,
    rs_send, rs_recv, z_send, z_recv, pg_send, pg_recv, l_send, l_recv, g_send, g_recv,
):
    g = lax.axis_index("grp")
    s = lax.axis_index("shard")
    zh, y = g // NY, g % NY
    c = s % NC
    chip = s // NC
    x, z = chip // NZ, chip % NZ

    def at(chip_to):
        return (g, chip_to * NC + c)

    right = at((x + 1) % NX * NZ + z)
    left = at((x + NX - 1) % NX * NZ + z)
    partner = (g, chip * NC + (1 - c))

    def remote(src, dst, send, recv, to):
        return pltpu.make_async_remote_copy(
            src_ref=src, dst_ref=dst, send_sem=send, recv_sem=recv, device_id=to, device_id_type=MESH
        )

    whole = pltpu.make_async_copy(tables_ref, win.at[:, pl.ds(0, WIN)], local_sem.at[0])
    again = pltpu.make_async_copy(tables_ref.at[:, pl.ds(0, HOT)], win.at[:, pl.ds(WIN, HOT)], local_sem.at[1])
    whole.start()
    again.start()

    barrier = pltpu.get_barrier_semaphore()
    pl.semaphore_signal(barrier, inc=1, device_id=partner, device_id_type=MESH)
    for o in range(1, CHIPS):
        pl.semaphore_signal(barrier, inc=1, device_id=at((chip + o) % CHIPS), device_id_type=MESH)
    for o in range(1, GROUPS):
        pl.semaphore_signal(barrier, inc=1, device_id=((g + o) % GROUPS, s), device_id_type=MESH)
    pl.semaphore_wait(barrier, 1 + CHIPS - 1 + GROUPS - 1)

    idx_out = [
        remote(idx_ref, idxs.at[chip], idx_send.at[o - 1], idx_recv.at[chip], at((chip + o) % CHIPS))
        for o in range(1, CHIPS)
    ]
    for copy in idx_out:
        copy.start()
    vz_out = [
        remote(v0_ref, vs.at[x, z], vz_send.at[o - 1], vz_recv.at[z], at(x * NZ + (z + o) % NZ))
        for o in range(1, NZ)
    ]
    for copy in vz_out:
        copy.start()
    idxs[chip] = idx_ref[...]
    vs[x, z] = v0_ref[...]

    whole.wait()
    again.wait()
    for w in range(GROUPS):
        hot[pl.ds(c * OWN + w * HOT, HOT)] = win[w, pl.ds(starts_ref[w], HOT), :]
    mine = hot.at[pl.ds(c * OWN, OWN)]
    hot_out = remote(mine, mine, hot_sem.at[0], hot_sem.at[1], partner)
    hot_out.start()

    def turn_hot(half):
        def step(i, carry):
            at_row = pl.multiple_of(half * OWN + i * 128, 128)
            tile = hot[pl.ds(at_row, 128), :].T
            high, low = split_bf16(tile)
            hot_t[0:D, pl.ds(at_row, 128)] = high
            hot_t[D:, pl.ds(at_row, 128)] = low
            return carry

        lax.fori_loop(0, OWN // 128, step, 0, unroll=4)

    turn_hot(c)
    pre_dense[...] = jnp.dot(v0_ref[...].astype(BF16), dense_ref[...], preferred_element_type=F32)
    for o in range(1, CHIPS):
        k = (chip + o) % CHIPS
        remote(idx_ref, idxs.at[k], idx_send.at[o - 1], idx_recv.at[k], left).wait_recv()
    hot_out.wait_recv()
    turn_hot(1 - c)

    row_iota = lax.broadcasted_iota(I32, (256, B), 0).astype(F32).astype(BF16)

    rs_to = {0: right, 1: left, 2: left, 3: right, 6: right, 7: left}
    rs_slot = {0: 0, 1: 1, 2: 2, 3: 3, 6: 4, 7: 5}
    rs_out = {
        p: remote(part.at[p], rx.at[rs_slot[p]], rs_send.at[rs_slot[p]], rs_recv.at[rs_slot[p]], rs_to[p])
        for p in rs_slot
    }

    def pool_step(p, carry):
        h, q = p // 2, p % 2
        xx = (x + 2 + h * (1 + 2 * q)) % NX
        for b in range(2):
            rows = idxs[xx * NZ + 2 * q + b]
            local = rows[0:4] - chip * ROWS
            counts = rows[4:8].astype(F32).astype(BF16)
            many = [jnp.broadcast_to(counts[k : k + 1], (256, B)) for k in range(4)]

            def build(j, carry):
                near = jnp.clip(local - j * 256, -1, 256).astype(F32).astype(BF16)
                tile = jnp.zeros((256, B), BF16)
                for k in range(4):
                    tile = jnp.where(row_iota == near[k : k + 1], many[k], tile)
                et[pl.ds(pl.multiple_of(j * 256, 256), 256), pl.ds(pl.multiple_of(p * 256 + b * B, B), B)] = tile
                return carry

            lax.fori_loop(0, ROWS // 256, build, 0, unroll=2)
        both = jnp.dot(
            hot_t[...], et[:, pl.ds(pl.multiple_of(p * 256, 256), 256)], preferred_element_type=F32
        )
        summed = both[0:D] + both[D:]
        part[p, 0] = summed[:, 0:B]
        part[p, 1] = summed[:, B:]
        for k in rs_out:

            @pl.when(p == k)
            def _():
                if k >= 6:
                    rs_out[k - 6].wait_recv()
                    part[k] = part[k] + rx[k - 6]
                rs_out[k].start()

        return carry

    lax.fori_loop(0, 8, pool_step, 0)

    for o in range(1, NZ):
        k = (z + o) % NZ
        remote(v0_ref, vs.at[x, k], vz_send.at[o - 1], vz_recv.at[k], left).wait_recv()
    v_right = remote(vs.at[x], vs.at[x], vx_send.at[0], vx_recv.at[0], right)
    v_left = remote(vs.at[x], vs.at[x], vx_send.at[1], vx_recv.at[1], left)
    v_right.start()
    v_left.start()

    for q in range(2):
        a, b = (2, 4) if q == 0 else (3, 5)
        src = {2: 2, 4: 6, 3: 3, 5: 7}
        rs_out[src[a]].wait_recv()
        rs_out[src[b]].wait_recv()
        qz[pl.ds(2 * q, 2)] = part[4 + q] + rx[a] + rx[b]
    z_out = [
        remote(qz.at[(z + o) % NZ], zr.at[z], z_send.at[o - 1], z_recv.at[z], at(x * NZ + (z + o) % NZ))
        for o in range(1, NZ)
    ]
    for copy in z_out:
        copy.start()

    xl, xr = (x + NX - 1) % NX, (x + 1) % NX
    v_right.wait_recv()
    on_right = remote(vs.at[xl, pl.ds(0, 2)], vs.at[xl, pl.ds(0, 2)], vx_send.at[2], vx_recv.at[2], right)
    on_right.start()
    v_left.wait_recv()
    on_left = remote(vs.at[xr, pl.ds(2, 2)], vs.at[xr, pl.ds(2, 2)], vx_send.at[3], vx_recv.at[3], left)
    on_left.start()

    place_iota = lax.broadcasted_iota(I32, (OUT_ROWS, B), 0)
    for i in range(OWN // B):
        hit = place_iota == places_ref[:, i * B : (i + 1) * B]
        place_hot[:, i * B : (i + 1) * B] = jnp.where(hit, 1.0, 0.0).astype(BF16)

    pooled_t = qz[z]
    for o in range(1, NZ):
        k = (z + o) % NZ
        remote(qz.at[k], zr.at[k], z_send.at[o - 1], z_recv.at[k], left).wait_recv()
        pooled_t = pooled_t + zr[k]
    pooled = pooled_t.T

    v0 = v0_ref[...]
    pair_dots = jnp.sum(v0 * pooled, axis=1, keepdims=True)
    preact = pre_dense[...] + pair_dots * pairs_ref[...]
    gate = jax.nn.sigmoid(preact)
    pre_grad = cot_ref[...] * gate * (1.0 + preact * (1.0 - gate))
    pair_grad = jnp.sum(pre_grad * pairs_ref[...], axis=1, keepdims=True)
    pgs[chip] = jnp.broadcast_to(pair_grad, (B, B)).T[0:8]
    pg_out = [
        remote(pgs.at[chip], pgs.at[chip], pg_send.at[o - 1], pg_recv.at[chip], at((chip + o) % CHIPS))
        for o in range(1, CHIPS)
    ]
    for copy in pg_out:
        copy.start()
    act_ref[...] = (preact * gate).astype(BF16)
    bgrad_ref[...] = (
        lax.dot_general(
            pre_grad.astype(BF16), dense_ref[...], (((1,), (1,)), ((), ())), preferred_element_type=F32
        )
        + pair_grad * pooled
    )

    on_right.wait_recv()
    on_left.wait_recv()
    for o in range(1, CHIPS):
        k = (chip + o) % CHIPS
        remote(pgs.at[k], pgs.at[k], pg_send.at[o - 1], pg_recv.at[k], left).wait_recv()
    columns = pgs[...].reshape(CHIPS * 8, B).T
    for i in range(CHIPS):
        xi, zi = i // NZ, i % NZ
        q = zi // 2
        h = ((xi - x + 2 + NX) * (1 + 2 * q)) % 4
        row = pl.multiple_of((2 * h + q) * 256 + (zi % 2) * B, B)
        high, low = split_bf16(vs[xi, zi] * columns[:, 8 * i : 8 * i + 1])
        grads[pl.ds(row, B), 0:D] = high
        grads[pl.ds(row, B), D:] = low

    def row_grads(half, t):
        row = pl.multiple_of(half * OWN + t * NY * HOT, NY * HOT)
        both = jnp.dot(et[pl.ds(row, NY * HOT), :], grads[...], preferred_element_type=F32)
        return both[:, 0:D] + both[:, D:]

    l_out = [remote(lsend.at[i], lrecv.at[i], l_send.at[i], l_recv.at[i], partner) for i in range(ZH)]
    for i in range(ZH):
        lsend[i] = row_grads(1 - c, (zh + 1 + i) % ZH)
        l_out[i].start()
    g_out = []
    for i in range(ZH):
        t = (zh + 1 + i) % ZH
        total = row_grads(c, t)
        l_out[i].wait_recv()
        outb[i] = (total + lrecv[i]).reshape(NY, HOT, D)
        for o in range(1, NY + 1):
            k = (y + o) % NY
            if i == ZH - 1 and o == NY:
                continue
            copy = remote(outb.at[i, k], grecv.at[g], g_send.at[len(g_out)], g_recv.at[g], (t * NY + k, s))
            copy.start()
            g_out.append(copy)
    grecv[g] = outb[ZH - 1, y]
    for o in range(1, GROUPS):
        k = (g + o) % GROUPS
        remote(grecv.at[k], grecv.at[k], g_send.at[o - 1], g_recv.at[k], left).wait_recv()
    high, low = split_bf16(grecv[...].reshape(OWN, D))
    both = jnp.dot(place_hot[...], jnp.concatenate([high, low], axis=1), preferred_element_type=F32)
    tgrad_ref[...] = (both[:, 0:D] + both[:, D:])[0:WIN]

    hot_out.wait_send()
    for copy in (*idx_out, *vz_out, *rs_out.values(), v_right, v_left, on_right, on_left):
        copy.wait_send()
    for copy in (*z_out, *pg_out, *l_out, *g_out):
        copy.wait_send()


def on_device(bottom_out, lookups, starts, tables, top_dense, top_pairs, cotangent):
    g = lax.axis_index("grp")
    s = lax.axis_index("shard")
    picked = lookups[:, 0, :].T
    hot_index = picked // WIN * HOT + picked % WIN
    counts = jnp.sum((hot_index[:, None, :] == hot_index[None, :, :]).astype(I32), axis=1)
    idx = jnp.concatenate([hot_index, counts], axis=0)
    my_starts = lax.dynamic_slice(starts, (g, s * GROUPS), (1, GROUPS))[0]
    recv_starts = lax.dynamic_slice(starts, (0, s * GROUPS + g), (GROUPS, 1))
    places = ((recv_starts + jnp.arange(HOT, dtype=I32)[None, :]) % WIN).reshape(1, OWN)
    vmem = pl.BlockSpec(memory_space=pltpu.VMEM)
    dma = pltpu.SemaphoreType.DMA
    act, bgrad, tgrad = pl.pallas_call(
        kernel,
        out_shape=(
            jax.ShapeDtypeStruct((B, 1024), BF16),
            jax.ShapeDtypeStruct((B, D), F32),
            jax.ShapeDtypeStruct((WIN, D), F32),
        ),
        in_specs=[pl.BlockSpec(memory_space=pltpu.SMEM)] + [vmem] * 6 + [pl.BlockSpec(memory_space=pl.ANY)],
        out_specs=(vmem, vmem, vmem),
        scratch_shapes=[
            pltpu.VMEM((GROUPS, PAD, D), F32),
            pltpu.VMEM((ROWS, D), F32),
            pltpu.VMEM((2 * D, ROWS), BF16),
            pltpu.VMEM((CHIPS, 8, B), I32),
            pltpu.VMEM((ROWS, CHIPS * B), BF16),
            pltpu.VMEM((8, 2, D, B), F32),
            pltpu.VMEM((6, 2, D, B), F32),
            pltpu.VMEM((NZ, D, B), F32),
            pltpu.VMEM((NZ, D, B), F32),
            pltpu.VMEM((NX, NZ, B, D), F32),
            pltpu.VMEM((CHIPS, 8, B), F32),
            pltpu.VMEM((CHIPS * B, 2 * D), BF16),
            pltpu.VMEM((B, 1024), F32),
            pltpu.VMEM((ZH, NY * HOT, D), F32),
            pltpu.VMEM((ZH, NY * HOT, D), F32),
            pltpu.VMEM((ZH, NY, HOT, D), F32),
            pltpu.VMEM((GROUPS, HOT, D), F32),
            pltpu.VMEM((OUT_ROWS, OWN), BF16),
            dma((2,)), dma((2,)), dma((CHIPS - 1,)), dma((CHIPS,)), dma((NZ - 1,)), dma((NZ,)), dma((4,)), dma((4,)),
            dma((6,)), dma((6,)), dma((NZ - 1,)), dma((NZ,)), dma((CHIPS - 1,)), dma((CHIPS,)),
            dma((ZH,)), dma((ZH,)), dma((GROUPS - 1,)), dma((GROUPS,)),
        ],
        compiler_params=pltpu.CompilerParams(
            collective_id=0, has_side_effects=True, vmem_limit_bytes=60 * 1024 * 1024
        ),
    )(
        my_starts, idx, places, bottom_out.astype(F32), top_dense, top_pairs, cotangent,
        tables.reshape(GROUPS, WIN, D),
    )
    return act, bgrad, tgrad[None, None]


def solution(mesh):
    in_specs = (
        P(("grp", "shard"), None),
        P(("grp", "shard"), None, None),
        P(),
        P(None, "shard", None),
        P(),
        P(),
        P(("grp", "shard"), None),
    )
    out_specs = (
        P(("grp", "shard"), None),
        P(("grp", "shard"), None),
        P(None, "shard", "grp", None),
    )
    return jax.shard_map(
        on_device, mesh=mesh, in_specs=in_specs, out_specs=out_specs, check_vma=False
    )
```

time: 1080 us -> 109 us (0.10)
  local copies, waits for them, and re-layouts: 685 us -> 6.49 us
  other arithmetic: 201 us -> 3.4 us
  Pallas kernels: 0 us -> 98.5 us
  waiting for transfers between devices: 78.8 us -> 0 us
  blocking collectives: 73.5 us -> 0 us
  starting transfers between devices: 32.6 us -> 0 us
    gather x12 -> x0, local copies, waits for them, and re-layouts: 661 us -> none  [the longest x8 653 us: pool_step(): fetched = tables[table_ids, jnp.clip(local, 0, span_rows - 1)]]
    while x32 -> x0, other arithmetic: 144 us -> none
    pallas_call x0 -> x1, Pallas kernels: none -> 98.5 us  [on_device(): pl.pallas_call(kernel, out_shape=(jax.ShapeDtypeStruct((B, 1024), BF16),...]
    all_to_all x3 -> x0, waiting for transfers between devices: 78.8 us -> none  [the longest x2 56.9 us: sent_to_all(): lax.all_to_all(jnp.broadcast_to(value[None], (size, *value.shape)), axis,...]
    all_to_all x1 -> x0, blocking collectives: 73.5 us -> none  [sum_at_owner(): lax.all_to_all(blocks, axis, split_axis=0, concat_axis=0, tiled=True)]
    all_to_all x3 -> x0, starting transfers between devices: 32.6 us -> none  [the longest x2 18.6 us: sent_to_all(): lax.all_to_all(jnp.broadcast_to(value[None], (size, *value.shape)), axis,...]
    reduce_sum x10 -> x1, other arithmetic: 25.3 us -> 0.02 us  [on_device(): jnp.sum((hot_index[:, None, :] == hot_index[None, :, :]).astype(I32), axi...]
    select_n x11 -> x1, other arithmetic: 19.2 us -> 0.6 us  [on_device(): (recv_starts + jnp.arange(HOT, dtype=I32)[None, :]) % WIN]
  transfers between devices with their start and end apart: 3 -> 0, of which waited for: 3 -> 0; matrix products, arithmetic and copies ran while one was open for 0% -> 0% of each run, Pallas kernels for 0% -> 0%
where the time goes in v1:
time: 109 us
  Pallas kernels  98.5 us (90%)
  local copies, waits for them, and re-layouts  6.49 us (6%)
  other arithmetic  3.4 us (3%)
    pallas_call x1, Pallas kernels, on_device(): pl.pallas_call(kernel, out_shape=(jax.ShapeDtypeStruct((B, 1024), BF16),...  98.5 us
    unnamed x5, local copies, waits for them, and re-layouts  5.61 us

profile of v1, /device:TPU:1, one launch (start us, length us, event | category | flops | bytes accessed | tf_op | source)
XLA Modules:
  0.0 109.0 jit_solution(17051560177469812713)
XLA Ops:
  0.6 0.0 copy-start
  0.7 0.9 copy-done
  1.5 0.6 dynamic-slice_bitcast_fusion.starts_ref
  2.1 0.2 dynamic-slice_reduce_fusion
  2.3 0.7 fusion.1
  3.0 0.6 pad_add_fusion.idx_ref
  3.6 0.1 add_remainder_fusion
  3.7 0.1 rem.47
  3.8 0.6 and_select_fusion.places_ref
  4.4 1.4 %convert_element_type.7.v0_ref = f32[128,128]{1,0:T(8,128)} convert(bf16[128,128]{1,0:T(8,128)(2,1)} %param.7) | non-fusion elementwise | flops 16384 | bytes 98304 | tf_op jit(solution)/shard_map/convert_element_type | solution.py:318
  5.8 98.5 %shard_map.94 = (bf16[128,1024]{1,0:T(8,128)(2,1)}, f32[128,128]{1,0:T(8,128)}, f32[328,128]{1,0:T(8,128)}) custom-call(s32[24]{0:T(128)} %dynamic-slice_bitcast_fusion.starts_ref, s32[8,128]{1,0:T(8,128)} %pad_add_fusion.idx_ref, s32[1,1536]{1,0:T(1,128)} %and_select_fusion.places_ref, f32[128,128]{1,0:T(8,128)} %convert_element_type.7.v0_ref, ...), custom_call_target="tpu_custom_call" | custom-call | tf_op jit(solution)/shard_map/pallas_call | solution.py:282
  104.3 1.7 %copy.13 = bf16[128,1024]{1,0:T(8,128)(2,1)} copy(bf16[128,1024]{1,0:T(8,128)(2,1)} %get-tuple-element.12) | data formatting | bytes 524288
  106.0 1.5 %copy.14 = f32[128,128]{1,0:T(8,128)} copy(f32[128,128]{1,0:T(8,128)} %get-tuple-element.13) | data formatting | bytes 131072
  107.4 1.6 %copy.15 = f32[1,1,328,128]{3,2,1,0:T(8,128)} copy(f32[1,1,328,128]{3,2,1,0:T(8,128)} %bitcast.29) | data formatting | bytes 335872
  (1 shorter events, 0.0 us)
Async XLA Ops:
  0.6 0.9 copy-start

commit v2 on v1

v2 whole, which is shorter than its diff:
```python
import jax
import jax.numpy as jnp
from jax import lax
from jax.experimental import pallas as pl
from jax.experimental.pallas import tpu as pltpu
from jax.sharding import PartitionSpec as P

HOT = 64
WIN = 328
NX, NZ, NC = 4, 4, 2
ZH, NY = 3, 8
CHIPS = NX * NZ
GROUPS = ZH * NY
B = 128
D = 128
OWN = GROUPS * HOT
ROWS = NC * OWN
PAD = WIN + HOT
OUT_ROWS = 336
F32, BF16, I32 = jnp.float32, jnp.bfloat16, jnp.int32
MESH = pl.DeviceIdType.MESH


def split_bf16(value):
    high = value.astype(BF16)
    return high, (value - high.astype(F32)).astype(BF16)


def kernel(
    bottom_hbm, lookups_hbm, pairs_hbm, starts_ref, tables_ref, dense_hbm, cot_hbm,
    act_ref, bgrad_ref, tgrad_ref,
    bottom_ref, lookups_ref, pairs_ref, dense_ref, cot_ref, start_of, win, hot, hot_t, idxs, et_a, et_b, part, rx, qz, zr, vs, pgs, grads, pre_dense, lsend, lrecv, outb, grecv, place_hot,
    local_sem, hot_sem, idx_send, idx_recv, vz_send, vz_recv, vx_send, vx_recv,
    rs_send, rs_recv, z_send, z_recv, pg_send, pg_recv, l_send, l_recv, g_send, g_recv,
):
    g = lax.axis_index("grp")
    s = lax.axis_index("shard")
    zh, y = g // NY, g % NY
    et = (et_a, et_b)
    c = s % NC
    chip = s // NC
    x, z = chip // NZ, chip % NZ

    def at(chip_to):
        return (g, chip_to * NC + c)

    right = at((x + 1) % NX * NZ + z)
    left = at((x + NX - 1) % NX * NZ + z)
    partner = (g, chip * NC + (1 - c))

    def remote(src, dst, send, recv, to):
        return pltpu.make_async_remote_copy(
            src_ref=src, dst_ref=dst, send_sem=send, recv_sem=recv, device_id=to, device_id_type=MESH
        )

    first = (s * GROUPS // 128 - s // 27) * 128
    starts_in = pltpu.make_async_copy(starts_ref.at[:, pl.ds(pl.multiple_of(first, 128), 256)], start_of, local_sem.at[2])
    whole = pltpu.make_async_copy(tables_ref, win.at[:, pl.ds(0, WIN)], local_sem.at[0])
    again = pltpu.make_async_copy(tables_ref.at[:, pl.ds(0, HOT)], win.at[:, pl.ds(WIN, HOT)], local_sem.at[1])
    dense_in = pltpu.make_async_copy(dense_hbm, dense_ref, local_sem.at[3])
    cot_in = pltpu.make_async_copy(cot_hbm, cot_ref, local_sem.at[4])
    lookups_in = pltpu.make_async_copy(lookups_hbm, lookups_ref, local_sem.at[5])
    bottom_in = pltpu.make_async_copy(bottom_hbm, bottom_ref, local_sem.at[6])
    pairs_in = pltpu.make_async_copy(pairs_hbm, pairs_ref, local_sem.at[7])
    for copy in (lookups_in, bottom_in, starts_in, whole, again, dense_in, cot_in, pairs_in):
        copy.start()

    barrier = pltpu.get_barrier_semaphore()
    pl.semaphore_signal(barrier, inc=1, device_id=partner, device_id_type=MESH)
    for o in range(1, CHIPS):
        pl.semaphore_signal(barrier, inc=1, device_id=at((chip + o) % CHIPS), device_id_type=MESH)
    for o in range(1, GROUPS):
        pl.semaphore_signal(barrier, inc=1, device_id=((g + o) % GROUPS, s), device_id_type=MESH)

    lookups_in.wait()
    picked = lookups_ref[...]
    window = ((picked.astype(F32) + 0.5) * (1.0 / WIN)).astype(I32)
    hot_index = picked - window * (WIN - HOT)
    counts = jnp.zeros((4, B), I32)
    for k in range(4):
        counts = counts + jnp.where(hot_index == hot_index[k : k + 1], 1, 0)
    idxs[chip, 0:4] = hot_index
    idxs[chip, 4:8] = counts
    bottom_in.wait()
    vs[x, z] = bottom_ref[...].astype(F32)
    starts_in.wait()
    whole.wait()
    again.wait()
    for w in range(GROUPS):
        hot[pl.ds(c * OWN + w * HOT, HOT)] = win[w, pl.ds(start_of[g, s * GROUPS - first + w], HOT), :]
    pl.semaphore_wait(barrier, 1 + CHIPS - 1 + GROUPS - 1)

    idx_out = [
        remote(idxs.at[chip], idxs.at[chip], idx_send.at[o - 1], idx_recv.at[chip], at((chip + o) % CHIPS))
        for o in range(1, CHIPS)
    ]
    for copy in idx_out:
        copy.start()
    mine = hot.at[pl.ds(c * OWN, OWN)]
    hot_out = remote(mine, mine, hot_sem.at[0], hot_sem.at[1], partner)
    hot_out.start()
    vz_out = [
        remote(vs.at[x, z], vs.at[x, z], vz_send.at[o - 1], vz_recv.at[z], at(x * NZ + (z + o) % NZ))
        for o in range(1, NZ)
    ]
    for copy in vz_out:
        copy.start()

    def turn_hot(half):
        def step(i, carry):
            at_row = pl.multiple_of(half * OWN + i * 128, 128)
            tile = hot[pl.ds(at_row, 128), :].T
            high, low = split_bf16(tile)
            hot_t[half * GROUPS // 2 + i, 0:D] = high
            hot_t[half * GROUPS // 2 + i, D:] = low
            return carry

        lax.fori_loop(0, OWN // 128, step, 0, unroll=4)

    turn_hot(c)
    dense_in.wait()
    pre_dense[...] = jnp.dot(bottom_ref[...], dense_ref[...], preferred_element_type=F32)
    for o in range(1, CHIPS):
        k = (chip + o) % CHIPS
        remote(idxs.at[k], idxs.at[k], idx_send.at[o - 1], idx_recv.at[k], left).wait_recv()
    hot_out.wait_recv()
    turn_hot(1 - c)

    row_iota = lax.broadcasted_iota(I32, (256, B), 0).astype(F32).astype(BF16)

    rs_to = {0: right, 1: left, 2: left, 3: right, 6: right, 7: left}
    rs_slot = {0: 0, 1: 1, 2: 2, 3: 3, 6: 4, 7: 5}
    rs_out = {
        p: remote(part.at[p], rx.at[rs_slot[p]], rs_send.at[rs_slot[p]], rs_recv.at[rs_slot[p]], rs_to[p])
        for p in rs_slot
    }

    def build(h, q):
        xx = (x + 2 + h * (1 + 2 * q)) % NX
        for b in range(2):
            rows = idxs[xx * NZ + 2 * q + b]
            local = rows[0:4] - chip * ROWS
            counts = rows[4:8].astype(F32).astype(BF16)
            for j in range(ROWS // 256):
                near = jnp.clip(local - j * 256, -1, 256).astype(F32).astype(BF16)
                tile = jnp.zeros((256, B), BF16)
                for k in range(4):
                    tile = jnp.where(row_iota == near[k : k + 1], counts[k : k + 1], tile)
                et[q][2 * h + b, j] = tile

    def pool(h, q):
        both = jnp.dot(
            jnp.concatenate([hot_t[i] for i in range(ROWS // 128)], axis=1),
            jnp.concatenate([et[q][2 * h + b].reshape(ROWS, B) for b in range(2)], axis=1),
            preferred_element_type=F32,
        )
        summed = both[0:D] + both[D:]
        part[2 * h + q, 0] = summed[:, 0:B]
        part[2 * h + q, 1] = summed[:, B:]

    def pass_on(h, q):
        for k in rs_out:
            if k % 2 == q:

                @pl.when(h == k // 2)
                def _():
                    if k >= 6:
                        rs_out[k - 6].wait_recv()
                        part[k] = part[k] + rx[k - 6]
                    rs_out[k].start()

    build(0, 0)

    def pool_step(h, carry):
        build(h, 1)
        pool(h, 0)
        pass_on(h, 0)
        build((h + 1) % 4, 0)
        pool(h, 1)
        pass_on(h, 1)
        return carry

    lax.fori_loop(0, 4, pool_step, 0)

    for o in range(1, NZ):
        k = (z + o) % NZ
        remote(vs.at[x, k], vs.at[x, k], vz_send.at[o - 1], vz_recv.at[k], left).wait_recv()
    v_right = remote(vs.at[x], vs.at[x], vx_send.at[0], vx_recv.at[0], right)
    v_left = remote(vs.at[x], vs.at[x], vx_send.at[1], vx_recv.at[1], left)
    v_right.start()
    v_left.start()

    for q in range(2):
        a, b = (2, 4) if q == 0 else (3, 5)
        src = {2: 2, 4: 6, 3: 3, 5: 7}
        rs_out[src[a]].wait_recv()
        rs_out[src[b]].wait_recv()
        qz[pl.ds(2 * q, 2)] = part[4 + q] + rx[a] + rx[b]
    z_out = [
        remote(qz.at[(z + o) % NZ], zr.at[z], z_send.at[o - 1], z_recv.at[z], at(x * NZ + (z + o) % NZ))
        for o in range(1, NZ)
    ]
    for copy in z_out:
        copy.start()

    xl, xr = (x + NX - 1) % NX, (x + 1) % NX
    v_right.wait_recv()
    on_right = remote(vs.at[xl, pl.ds(0, 2)], vs.at[xl, pl.ds(0, 2)], vx_send.at[2], vx_recv.at[2], right)
    on_right.start()
    v_left.wait_recv()
    on_left = remote(vs.at[xr, pl.ds(2, 2)], vs.at[xr, pl.ds(2, 2)], vx_send.at[3], vx_recv.at[3], left)
    on_left.start()

    place_iota = lax.broadcasted_iota(I32, (OUT_ROWS, B), 0)
    lane = lax.broadcasted_iota(I32, (1, B), 1)
    column = s * GROUPS - first + g
    for i in range(OWN // B):
        place = lane % HOT + jnp.where(lane < HOT, start_of[2 * i, column], start_of[2 * i + 1, column])
        place = jnp.where(place >= WIN, place - WIN, place)
        place_hot[i] = jnp.where(place_iota == place, 1.0, 0.0).astype(BF16)

    pooled_t = qz[z]
    for o in range(1, NZ):
        k = (z + o) % NZ
        remote(qz.at[k], zr.at[k], z_send.at[o - 1], z_recv.at[k], left).wait_recv()
        pooled_t = pooled_t + zr[k]
    pooled = pooled_t.T

    v0 = bottom_ref[...].astype(F32)
    cot_in.wait()
    pairs_in.wait()
    pair_dots = jnp.sum(v0 * pooled, axis=1, keepdims=True)
    preact = pre_dense[...] + pair_dots * pairs_ref[...]
    gate = jax.nn.sigmoid(preact)
    pre_grad = cot_ref[...] * gate * (1.0 + preact * (1.0 - gate))
    pair_grad = jnp.sum(pre_grad * pairs_ref[...], axis=1, keepdims=True)
    pgs[chip] = jnp.broadcast_to(pair_grad, (B, B)).T[0:8]
    pg_out = [
        remote(pgs.at[chip], pgs.at[chip], pg_send.at[o - 1], pg_recv.at[chip], at((chip + o) % CHIPS))
        for o in range(1, CHIPS)
    ]
    for copy in pg_out:
        copy.start()
    act_ref[...] = (preact * gate).astype(BF16)
    bgrad_ref[...] = (
        lax.dot_general(
            pre_grad.astype(BF16), dense_ref[...], (((1,), (1,)), ((), ())), preferred_element_type=F32
        )
        + pair_grad * pooled
    )

    on_right.wait_recv()
    on_left.wait_recv()
    for o in range(1, CHIPS):
        k = (chip + o) % CHIPS
        remote(pgs.at[k], pgs.at[k], pg_send.at[o - 1], pg_recv.at[k], left).wait_recv()
    columns = pgs[...].reshape(CHIPS * 8, B).T
    for i in range(CHIPS):
        xi, zi = i // NZ, i % NZ
        q = zi // 2
        h = ((xi - x + 2 + NX) * (1 + 2 * q)) % 4
        slot = q * 8 + 2 * h + zi % 2
        high, low = split_bf16(vs[xi, zi] * columns[:, 8 * i : 8 * i + 1])
        grads[0, slot] = high
        grads[1, slot] = low

    half_to = y // 4

    def spans(i):
        if i == 2:
            return [(zh, 0), (zh, 1)]
        block = (half_to + 1 + i) % 2
        return [((zh + 1) % ZH, block), ((zh + 2) % ZH, block)]

    def row_grads(half, i):
        rows = [
            jnp.concatenate([et[k // 8][k % 8, half * (OWN // 256) + t * 2 + block] for k in range(CHIPS)], axis=1)
            for t, block in spans(i)
        ]
        right_side = jnp.concatenate([grads[k].reshape(CHIPS * B, D) for k in range(2)], axis=1)
        both = jnp.dot(jnp.concatenate(rows, axis=0), right_side, preferred_element_type=F32)
        return both[:, 0:D] + both[:, D:]

    l_out = [remote(lsend.at[i], lrecv.at[i], l_send.at[i], l_recv.at[i], partner) for i in range(3)]
    g_out = []
    for i in range(3):
        lsend[i] = row_grads(1 - c, i)
        l_out[i].start()
        total = row_grads(c, i)
        l_out[i].wait_recv()
        outb[i] = (total + lrecv[i]).reshape(NY, HOT, D)
        if i < 2:
            (t, block), (u, _) = spans(i)
            order = [(zz, part_of * 4 + k, block * 4 + k) for k in range(4) for part_of, zz in ((0, t), (1, u))]
        else:
            order = [(zh, (y + o) % NY, (y + o) % NY) for o in range(1, NY)]
        for zz, k, yy in order:
            copy = remote(outb.at[i, k], grecv.at[g], g_send.at[len(g_out)], g_recv.at[g], (zz * NY + yy, s))
            copy.start()
            g_out.append(copy)
    grecv[g] = outb[2, y]
    for o in range(1, GROUPS):
        k = (g + o) % GROUPS
        remote(grecv.at[k], grecv.at[k], g_send.at[o - 1], g_recv.at[k], left).wait_recv()
    high, low = split_bf16(grecv[...].reshape(OWN, D))
    both = jnp.dot(
        jnp.concatenate([place_hot[i] for i in range(OWN // B)], axis=1),
        jnp.concatenate([high, low], axis=1),
        preferred_element_type=F32,
    )
    tgrad_ref[...] = (both[:, 0:D] + both[:, D:])[0:WIN]

    hot_out.wait_send()
    for copy in (*idx_out, *vz_out, *rs_out.values(), v_right, v_left, on_right, on_left):
        copy.wait_send()
    for copy in (*z_out, *pg_out, *l_out, *g_out):
        copy.wait_send()


def keep(*refs):
    for source, target in zip(refs[:3], refs[3:]):
        target[...] = source[...]


def on_device(bottom_out, lookups, starts, tables, top_dense, top_pairs, cotangent):
    vmem = pl.BlockSpec(memory_space=pltpu.VMEM)
    dma = pltpu.SemaphoreType.DMA
    hbm = pl.BlockSpec(memory_space=pltpu.HBM)
    shapes = (
        jax.ShapeDtypeStruct((B, 1024), BF16),
        jax.ShapeDtypeStruct((B, D), F32),
        jax.ShapeDtypeStruct((WIN, D), F32),
    )
    operands = (
        bottom_out, lookups[:, 0, :].T, top_pairs, starts, tables.reshape(GROUPS, WIN, D), top_dense, cotangent,
    )
    results = pl.pallas_call(
        kernel,
        out_shape=shapes,
        in_specs=[hbm] * 7,
        out_specs=(vmem, vmem, vmem),
        scratch_shapes=[
            pltpu.VMEM((B, D), BF16),
            pltpu.VMEM((4, B), I32),
            pltpu.VMEM((1, 1024), F32),
            pltpu.VMEM((D, 1024), BF16),
            pltpu.VMEM((B, 1024), F32),
            pltpu.SMEM((GROUPS, 256), I32),
            pltpu.VMEM((GROUPS, PAD, D), F32),
            pltpu.VMEM((ROWS, D), F32),
            pltpu.VMEM((ROWS // 128, 2 * D, 128), BF16),
            pltpu.VMEM((CHIPS, 8, B), I32),
            pltpu.VMEM((CHIPS // 2, ROWS // 256, 256, B), BF16),
            pltpu.VMEM((CHIPS // 2, ROWS // 256, 256, B), BF16),
            pltpu.VMEM((8, 2, D, B), F32),
            pltpu.VMEM((6, 2, D, B), F32),
            pltpu.VMEM((NZ, D, B), F32),
            pltpu.VMEM((NZ, D, B), F32),
            pltpu.VMEM((NX, NZ, B, D), F32),
            pltpu.VMEM((CHIPS, 8, B), F32),
            pltpu.VMEM((2, CHIPS, B, D), BF16),
            pltpu.VMEM((B, 1024), F32),
            pltpu.VMEM((ZH, NY * HOT, D), F32),
            pltpu.VMEM((ZH, NY * HOT, D), F32),
            pltpu.VMEM((ZH, NY, HOT, D), F32),
            pltpu.VMEM((GROUPS, HOT, D), F32),
            pltpu.VMEM((OWN // B, OUT_ROWS, B), BF16),
            dma((8,)), dma((2,)), dma((CHIPS - 1,)), dma((CHIPS,)), dma((NZ - 1,)), dma((NZ,)), dma((4,)), dma((4,)),
            dma((6,)), dma((6,)), dma((NZ - 1,)), dma((NZ,)), dma((CHIPS - 1,)), dma((CHIPS,)),
            dma((ZH,)), dma((ZH,)), dma((GROUPS - 1,)), dma((GROUPS,)),
        ],
        compiler_params=pltpu.CompilerParams(
            collective_id=0, has_side_effects=True, vmem_limit_bytes=38 * 1024 * 1024
        ),
    )(
        *(pltpu.with_memory_space_constraint(value, pltpu.HBM) for value in operands)
    )
    act, bgrad, tgrad = pl.pallas_call(
        keep,
        out_shape=shapes,
        in_specs=[vmem] * 3,
        out_specs=(vmem,) * 3,
        compiler_params=pltpu.CompilerParams(vmem_limit_bytes=4 * 1024 * 1024),
    )(*results)
    return act, bgrad, tgrad[None, None]


def solution(mesh):
    in_specs = (
        P(("grp", "shard"), None),
        P(("grp", "shard"), None, None),
        P(),
        P(None, "shard", None),
        P(),
        P(),
        P(("grp", "shard"), None),
    )
    out_specs = (
        P(("grp", "shard"), None),
        P(("grp", "shard"), None),
        P(None, "shard", "grp", None),
    )
    return jax.shard_map(
        on_device, mesh=mesh, in_specs=in_specs, out_specs=out_specs, check_vma=False
    )
```

time: 109 us -> 99 us (0.908)
  local copies, waits for them, and re-layouts: 6.49 us -> 0 us
  other arithmetic: 3.4 us -> 0 us
    unnamed x5 -> x0, local copies, waits for them, and re-layouts: 5.61 us -> none
    convert_element_type x1 -> x0, other arithmetic: 1.39 us -> none  [on_device(): bottom_out.astype(F32)]
    pallas_call x1 -> x2, Pallas kernels: 98.5 us -> 98.2 us  [the longest x1 97.4 us: on_device(): pl.pallas_call(kernel, out_shape=shapes, in_specs=[hbm] * 7, out_specs=(v...]
where the time goes in v2:
time: 99 us; the launch traced here: 98.9 us
  Pallas kernels  98.2 us (99%)
    pallas_call x1, Pallas kernels, on_device(): pl.pallas_call(kernel, out_shape=shapes, in_specs=[hbm] * 7, out_specs=(v...  97.4 us

profile of v2, /device:TPU:1, one launch (start us, length us, event | category | flops | bytes accessed | tf_op | source)
XLA Modules:
  0.0 98.9 jit_solution(9812536696162561886)
XLA Ops:
  0.6 97.4 %shard_map.94 = (bf16[128,1024]{1,0:T(8,128)(2,1)S(1)}, f32[128,128]{1,0:T(8,128)S(1)}, f32[328,128]{1,0:T(8,128)S(1)}) custom-call(bf16[128,128]{1,0:T(8,128)(2,1)} %bottom_hbm.1, s32[4,128]{1,0:T(4,128)} %bitcast.6, f32[1,1024]{1,0:T(1,128)} %pairs_hbm.1, s32[24,768]{1,0:T(8,128)} %starts_ref.1, f32[24,328,128]{2,1,0:T(8,128)} %bitcast.5, ...), custom_call_target="tpu_custom_call" | custom-call | tf_op jit(solution)/shard_map/pallas_call | solution.py:337
  98.1 0.8 shard_map.95

commit v3 on v2

--- a/solution.py
+++ b/solution.py
@@ -83,11 +83,6 @@
     idxs[chip, 4:8] = counts
     bottom_in.wait()
     vs[x, z] = bottom_ref[...].astype(F32)
-    starts_in.wait()
-    whole.wait()
-    again.wait()
-    for w in range(GROUPS):
-        hot[pl.ds(c * OWN + w * HOT, HOT)] = win[w, pl.ds(start_of[g, s * GROUPS - first + w], HOT), :]
     pl.semaphore_wait(barrier, 1 + CHIPS - 1 + GROUPS - 1)
 
     idx_out = [
@@ -96,15 +91,14 @@
     ]
     for copy in idx_out:
         copy.start()
+    starts_in.wait()
+    whole.wait()
+    again.wait()
+    for w in range(GROUPS):
+        hot[pl.ds(c * OWN + w * HOT, HOT)] = win[w, pl.ds(start_of[g, s * GROUPS - first + w], HOT), :]
     mine = hot.at[pl.ds(c * OWN, OWN)]
     hot_out = remote(mine, mine, hot_sem.at[0], hot_sem.at[1], partner)
     hot_out.start()
-    vz_out = [
-        remote(vs.at[x, z], vs.at[x, z], vz_send.at[o - 1], vz_recv.at[z], at(x * NZ + (z + o) % NZ))
-        for o in range(1, NZ)
-    ]
-    for copy in vz_out:
-        copy.start()
 
     def turn_hot(half):
         def step(i, carry):
@@ -123,20 +117,29 @@
     for o in range(1, CHIPS):
         k = (chip + o) % CHIPS
         remote(idxs.at[k], idxs.at[k], idx_send.at[o - 1], idx_recv.at[k], left).wait_recv()
+    vz_out = [
+        remote(vs.at[x, z], vs.at[x, z], vz_send.at[o - 1], vz_recv.at[z], at(x * NZ + (z + o) % NZ))
+        for o in range(1, NZ)
+    ]
+    for copy in vz_out:
+        copy.start()
     hot_out.wait_recv()
     turn_hot(1 - c)
 
     row_iota = lax.broadcasted_iota(I32, (256, B), 0).astype(F32).astype(BF16)
 
-    rs_to = {0: right, 1: left, 2: left, 3: right, 6: right, 7: left}
-    rs_slot = {0: 0, 1: 1, 2: 2, 3: 3, 6: 4, 7: 5}
-    rs_out = {
-        p: remote(part.at[p], rx.at[rs_slot[p]], rs_send.at[rs_slot[p]], rs_recv.at[rs_slot[p]], rs_to[p])
-        for p in rs_slot
-    }
+    rs_to = {0: right, 1: left, 2: left, 3: right, 4: right, 5: left}
+    rs_out = {p: remote(part.at[p], rx.at[p], rs_send.at[p], rs_recv.at[p], to) for p, to in rs_to.items()}
+
+    def x_of(h, q):
+        return (x + (2 + h + h // 2 * (2 * h - 3)) * (1 + 2 * q)) % NX
+
+    def turn_of(xx, q):
+        m = ((xx - x + NX) * (1 + 2 * q) + 2) % NX
+        return m + m // 2 * (5 - 2 * m)
 
     def build(h, q):
-        xx = (x + 2 + h * (1 + 2 * q)) % NX
+        xx = x_of(h, q)
         for b in range(2):
             rows = idxs[xx * NZ + 2 * q + b]
             local = rows[0:4] - chip * ROWS
@@ -164,10 +167,19 @@
 
                 @pl.when(h == k // 2)
                 def _():
-                    if k >= 6:
-                        rs_out[k - 6].wait_recv()
-                        part[k] = part[k] + rx[k - 6]
+                    if k >= 4:
+                        rs_out[k - 4].wait_recv()
+                        part[k] = part[k] + rx[k - 4]
                     rs_out[k].start()
+                    if k == 5:
+                        for o in range(1, NZ):
+                            kz = (z + o) % NZ
+                            remote(vs.at[x, kz], vs.at[x, kz], vz_send.at[o - 1], vz_recv.at[kz], left).wait_recv()
+                        v_right.start()
+                        v_left.start()
+
+    v_right = remote(vs.at[x], vs.at[x], vx_send.at[0], vx_recv.at[0], right)
+    v_left = remote(vs.at[x], vs.at[x], vx_send.at[1], vx_recv.at[1], left)
 
     build(0, 0)
 
@@ -182,20 +194,11 @@
 
     lax.fori_loop(0, 4, pool_step, 0)
 
-    for o in range(1, NZ):
-        k = (z + o) % NZ
-        remote(vs.at[x, k], vs.at[x, k], vz_send.at[o - 1], vz_recv.at[k], left).wait_recv()
-    v_right = remote(vs.at[x], vs.at[x], vx_send.at[0], vx_recv.at[0], right)
-    v_left = remote(vs.at[x], vs.at[x], vx_send.at[1], vx_recv.at[1], left)
-    v_right.start()
-    v_left.start()
-
     for q in range(2):
         a, b = (2, 4) if q == 0 else (3, 5)
-        src = {2: 2, 4: 6, 3: 3, 5: 7}
-        rs_out[src[a]].wait_recv()
-        rs_out[src[b]].wait_recv()
-        qz[pl.ds(2 * q, 2)] = part[4 + q] + rx[a] + rx[b]
+        rs_out[a].wait_recv()
+        rs_out[b].wait_recv()
+        qz[pl.ds(2 * q, 2)] = part[6 + q] + rx[a] + rx[b]
     z_out = [
         remote(qz.at[(z + o) % NZ], zr.at[z], z_send.at[o - 1], z_recv.at[z], at(x * NZ + (z + o) % NZ))
         for o in range(1, NZ)
@@ -258,8 +261,7 @@
     for i in range(CHIPS):
         xi, zi = i // NZ, i % NZ
         q = zi // 2
-        h = ((xi - x + 2 + NX) * (1 + 2 * q)) % 4
-        slot = q * 8 + 2 * h + zi % 2
+        slot = q * 8 + 2 * turn_of(xi, q) + zi % 2
         high, low = split_bf16(vs[xi, zi] * columns[:, 8 * i : 8 * i + 1])
         grads[0, slot] = high
         grads[1, slot] = low
@@ -291,7 +293,9 @@
         outb[i] = (total + lrecv[i]).reshape(NY, HOT, D)
         if i < 2:
             (t, block), (u, _) = spans(i)
-            order = [(zz, part_of * 4 + k, block * 4 + k) for k in range(4) for part_of, zz in ((0, t), (1, u))]
+            order = [
+                (zz, part_of * 4 + (y + k) % 4, block * 4 + (y + k) % 4) for k in range(4) for part_of, zz in ((0, t), (1, u))
+            ]
         else:
             order = [(zh, (y + o) % NY, (y + o) % NY) for o in range(1, NY)]
         for zz, k, yy in order:

time: 99 us -> 89.6 us (0.905)
  Pallas kernels: 98.2 us -> 88.8 us
    pallas_call x1, Pallas kernels: 97.4 us -> 88 us  [on_device(): pl.pallas_call(kernel, out_shape=shapes, in_specs=[hbm] * 7, out_specs=(v...]
where the time goes in v3:
time: 89.6 us; the launch traced here: 89.5 us
  Pallas kernels  88.8 us (99%)
    pallas_call x1, Pallas kernels, on_device(): pl.pallas_call(kernel, out_shape=shapes, in_specs=[hbm] * 7, out_specs=(v...  88 us

profile of v3, /device:TPU:1, one launch (start us, length us, event | category | flops | bytes accessed | tf_op | source)
XLA Modules:
  0.0 89.5 jit_solution(15801393437565900143)
XLA Ops:
  0.6 88.0 %shard_map.94 = (bf16[128,1024]{1,0:T(8,128)(2,1)S(1)}, f32[128,128]{1,0:T(8,128)S(1)}, f32[328,128]{1,0:T(8,128)S(1)}) custom-call(bf16[128,128]{1,0:T(8,128)(2,1)} %bottom_hbm.1, s32[4,128]{1,0:T(4,128)} %bitcast.6, f32[1,1024]{1,0:T(1,128)} %pairs_hbm.1, s32[24,768]{1,0:T(8,128)} %starts_ref.1, f32[24,328,128]{2,1,0:T(8,128)} %bitcast.5, ...), custom_call_target="tpu_custom_call" | custom-call | tf_op jit(solution)/shard_map/pallas_call | solution.py:341
  88.6 0.8 shard_map.95

commit v4 on v3

--- a/solution.py
+++ b/solution.py
@@ -30,7 +30,7 @@
     bottom_hbm, lookups_hbm, pairs_hbm, starts_ref, tables_ref, dense_hbm, cot_hbm,
     act_ref, bgrad_ref, tgrad_ref,
     bottom_ref, lookups_ref, pairs_ref, dense_ref, cot_ref, start_of, win, hot, hot_t, idxs, et_a, et_b, part, rx, qz, zr, vs, pgs, grads, pre_dense, lsend, lrecv, outb, grecv, place_hot,
-    local_sem, hot_sem, idx_send, idx_recv, vz_send, vz_recv, vx_send, vx_recv,
+    local_sem, hot_sem, idx_send, idx_recv, vz_send, vz_recv, far_send, far_recv, vx_send, vx_recv,
     rs_send, rs_recv, z_send, z_recv, pg_send, pg_recv, l_send, l_recv, g_send, g_recv,
 ):
     g = lax.axis_index("grp")
@@ -91,6 +91,19 @@
     ]
     for copy in idx_out:
         copy.start()
+    vz_out = [
+        remote(vs.at[x, z], vs.at[x, z], vz_send.at[o - 1], vz_recv.at[z], at(x * NZ + (z + o) % NZ))
+        for o in range(1, NZ)
+    ]
+    for copy in vz_out:
+        copy.start()
+    x_far = (x + 2) % NX
+    far_out = remote(vs.at[x, z], vs.at[x, z], far_send.at[NZ - 1], far_recv.at[z], at(x_far * NZ + z))
+    far_out.start()
+    far_on = [
+        remote(vs.at[x_far, z], vs.at[x_far, z], far_send.at[o - 1], far_recv.at[z], at(x * NZ + (z + o) % NZ))
+        for o in range(1, NZ)
+    ]
     starts_in.wait()
     whole.wait()
     again.wait()
@@ -114,17 +127,14 @@
     turn_hot(c)
     dense_in.wait()
     pre_dense[...] = jnp.dot(bottom_ref[...], dense_ref[...], preferred_element_type=F32)
-    for o in range(1, CHIPS):
-        k = (chip + o) % CHIPS
-        remote(idxs.at[k], idxs.at[k], idx_send.at[o - 1], idx_recv.at[k], left).wait_recv()
-    vz_out = [
-        remote(vs.at[x, z], vs.at[x, z], vz_send.at[o - 1], vz_recv.at[z], at(x * NZ + (z + o) % NZ))
-        for o in range(1, NZ)
-    ]
-    for copy in vz_out:
-        copy.start()
     hot_out.wait_recv()
     turn_hot(1 - c)
+
+    def await_idx(k):
+        remote(idxs.at[k], idxs.at[k], idx_send.at[0], idx_recv.at[k], left).wait_recv()
+
+    for o in range(1, NZ):
+        await_idx(x * NZ + (z + o) % NZ)
 
     row_iota = lax.broadcasted_iota(I32, (256, B), 0).astype(F32).astype(BF16)
 
@@ -171,6 +181,10 @@
                         rs_out[k - 4].wait_recv()
                         part[k] = part[k] + rx[k - 4]
                     rs_out[k].start()
+                    if k == 0:
+                        remote(vs.at[x_far, z], vs.at[x_far, z], far_send.at[0], far_recv.at[z], left).wait_recv()
+                        for copy in far_on:
+                            copy.start()
                     if k == 5:
                         for o in range(1, NZ):
                             kz = (z + o) % NZ
@@ -181,12 +195,25 @@
     v_right = remote(vs.at[x], vs.at[x], vx_send.at[0], vx_recv.at[0], right)
     v_left = remote(vs.at[x], vs.at[x], vx_send.at[1], vx_recv.at[1], left)
 
+    for b in range(2):
+        await_idx(x_far * NZ + b)
     build(0, 0)
 
     def pool_step(h, carry):
+        @pl.when(h < 3)
+        def _():
+            for b in range(2):
+                await_idx(x_of(h, 1) * NZ + 2 + b)
+
         build(h, 1)
         pool(h, 0)
         pass_on(h, 0)
+
+        @pl.when(h < 2)
+        def _():
+            for b in range(2):
+                await_idx(x_of(h + 1, 0) * NZ + b)
+
         build((h + 1) % 4, 0)
         pool(h, 1)
         pass_on(h, 1)
@@ -205,14 +232,6 @@
     ]
     for copy in z_out:
         copy.start()
-
-    xl, xr = (x + NX - 1) % NX, (x + 1) % NX
-    v_right.wait_recv()
-    on_right = remote(vs.at[xl, pl.ds(0, 2)], vs.at[xl, pl.ds(0, 2)], vx_send.at[2], vx_recv.at[2], right)
-    on_right.start()
-    v_left.wait_recv()
-    on_left = remote(vs.at[xr, pl.ds(2, 2)], vs.at[xr, pl.ds(2, 2)], vx_send.at[3], vx_recv.at[3], left)
-    on_left.start()
 
     place_iota = lax.broadcasted_iota(I32, (OUT_ROWS, B), 0)
     lane = lax.broadcasted_iota(I32, (1, B), 1)
@@ -252,8 +271,11 @@
         + pair_grad * pooled
     )
 
-    on_right.wait_recv()
-    on_left.wait_recv()
+    v_right.wait_recv()
+    v_left.wait_recv()
+    for o in range(1, NZ):
+        k = (z + o) % NZ
+        remote(vs.at[x_far, k], vs.at[x_far, k], far_send.at[0], far_recv.at[k], left).wait_recv()
     for o in range(1, CHIPS):
         k = (chip + o) % CHIPS
         remote(pgs.at[k], pgs.at[k], pg_send.at[o - 1], pg_recv.at[k], left).wait_recv()
@@ -266,18 +288,12 @@
         grads[0, slot] = high
         grads[1, slot] = low
 
-    half_to = y // 4
-
-    def spans(i):
-        if i == 2:
-            return [(zh, 0), (zh, 1)]
-        block = (half_to + 1 + i) % 2
-        return [((zh + 1) % ZH, block), ((zh + 2) % ZH, block)]
+    parts = [(zh + 1 + z // 2) % ZH, (zh + 2 + 2 * (z // 2)) % ZH, zh]
 
     def row_grads(half, i):
         rows = [
             jnp.concatenate([et[k // 8][k % 8, half * (OWN // 256) + t * 2 + block] for k in range(CHIPS)], axis=1)
-            for t, block in spans(i)
+            for t, block in ((parts[i], 0), (parts[i], 1))
         ]
         right_side = jnp.concatenate([grads[k].reshape(CHIPS * B, D) for k in range(2)], axis=1)
         both = jnp.dot(jnp.concatenate(rows, axis=0), right_side, preferred_element_type=F32)
@@ -291,15 +307,11 @@
         total = row_grads(c, i)
         l_out[i].wait_recv()
         outb[i] = (total + lrecv[i]).reshape(NY, HOT, D)
-        if i < 2:
-            (t, block), (u, _) = spans(i)
-            order = [
-                (zz, part_of * 4 + (y + k) % 4, block * 4 + (y + k) % 4) for k in range(4) for part_of, zz in ((0, t), (1, u))
-            ]
-        else:
-            order = [(zh, (y + o) % NY, (y + o) % NY) for o in range(1, NY)]
-        for zz, k, yy in order:
-            copy = remote(outb.at[i, k], grecv.at[g], g_send.at[len(g_out)], g_recv.at[g], (zz * NY + yy, s))
+        for o in (1, 7, 2, 6, 3, 5, 4, 0):
+            if i == 2 and o == 0:
+                continue
+            k = (y + o) % NY
+            copy = remote(outb.at[i, k], grecv.at[g], g_send.at[len(g_out)], g_recv.at[g], (parts[i] * NY + k, s))
             copy.start()
             g_out.append(copy)
     grecv[g] = outb[2, y]
@@ -315,7 +327,7 @@
     tgrad_ref[...] = (both[:, 0:D] + both[:, D:])[0:WIN]
 
     hot_out.wait_send()
-    for copy in (*idx_out, *vz_out, *rs_out.values(), v_right, v_left, on_right, on_left):
+    for copy in (*idx_out, *vz_out, *rs_out.values(), v_right, v_left, far_out, *far_on):
         copy.wait_send()
     for copy in (*z_out, *pg_out, *l_out, *g_out):
         copy.wait_send()
@@ -369,7 +381,7 @@
             pltpu.VMEM((ZH, NY, HOT, D), F32),
             pltpu.VMEM((GROUPS, HOT, D), F32),
             pltpu.VMEM((OWN // B, OUT_ROWS, B), BF16),
-            dma((8,)), dma((2,)), dma((CHIPS - 1,)), dma((CHIPS,)), dma((NZ - 1,)), dma((NZ,)), dma((4,)), dma((4,)),
+            dma((8,)), dma((2,)), dma((CHIPS - 1,)), dma((CHIPS,)), dma((NZ - 1,)), dma((NZ,)), dma((NZ,)), dma((NZ,)), dma((2,)), dma((2,)),
             dma((6,)), dma((6,)), dma((NZ - 1,)), dma((NZ,)), dma((CHIPS - 1,)), dma((CHIPS,)),
             dma((ZH,)), dma((ZH,)), dma((GROUPS - 1,)), dma((GROUPS,)),
         ],

time: 89.6 us -> 87.4 us (0.975)
  Pallas kernels: 88.8 us -> 86.6 us
    pallas_call x1, Pallas kernels: 88 us -> 85.8 us  [on_device(): pl.pallas_call(kernel, out_shape=shapes, in_specs=[hbm] * 7, out_specs=(v...]
where the time goes in v4:
time: 87.4 us; the launch traced here: 87.2 us
  Pallas kernels  86.6 us (99%)
    pallas_call x1, Pallas kernels, on_device(): pl.pallas_call(kernel, out_shape=shapes, in_specs=[hbm] * 7, out_specs=(v...  85.8 us

profile of v4, /device:TPU:1, one launch (start us, length us, event | category | flops | bytes accessed | tf_op | source)
XLA Modules:
  0.0 87.2 jit_solution(9971358826319143044)
XLA Ops:
  0.6 85.8 %shard_map.94 = (bf16[128,1024]{1,0:T(8,128)(2,1)S(1)}, f32[128,128]{1,0:T(8,128)S(1)}, f32[328,128]{1,0:T(8,128)S(1)}) custom-call(bf16[128,128]{1,0:T(8,128)(2,1)} %bottom_hbm.1, s32[4,128]{1,0:T(4,128)} %bitcast.6, f32[1,1024]{1,0:T(1,128)} %pairs_hbm.1, s32[24,768]{1,0:T(8,128)} %starts_ref.1, f32[24,328,128]{2,1,0:T(8,128)} %bitcast.5, ...), custom_call_target="tpu_custom_call" | custom-call | tf_op jit(solution)/shard_map/pallas_call | solution.py:353
  86.4 0.8 shard_map.95

commit v5 on v4

--- a/solution.py
+++ b/solution.py
@@ -185,12 +185,6 @@
                         remote(vs.at[x_far, z], vs.at[x_far, z], far_send.at[0], far_recv.at[z], left).wait_recv()
                         for copy in far_on:
                             copy.start()
-                    if k == 5:
-                        for o in range(1, NZ):
-                            kz = (z + o) % NZ
-                            remote(vs.at[x, kz], vs.at[x, kz], vz_send.at[o - 1], vz_recv.at[kz], left).wait_recv()
-                        v_right.start()
-                        v_left.start()
 
     v_right = remote(vs.at[x], vs.at[x], vx_send.at[0], vx_recv.at[0], right)
     v_left = remote(vs.at[x], vs.at[x], vx_send.at[1], vx_recv.at[1], left)
@@ -226,12 +220,17 @@
         rs_out[a].wait_recv()
         rs_out[b].wait_recv()
         qz[pl.ds(2 * q, 2)] = part[6 + q] + rx[a] + rx[b]
-    z_out = [
-        remote(qz.at[(z + o) % NZ], zr.at[z], z_send.at[o - 1], z_recv.at[z], at(x * NZ + (z + o) % NZ))
-        for o in range(1, NZ)
-    ]
-    for copy in z_out:
-        copy.start()
+        for k in (2 * q, 2 * q + 1):
+
+            @pl.when(z != k)
+            def _():
+                remote(qz.at[k], zr.at[z], z_send.at[k], z_recv.at[z], at(x * NZ + k)).start()
+
+    for o in range(1, NZ):
+        k = (z + o) % NZ
+        remote(vs.at[x, k], vs.at[x, k], vz_send.at[o - 1], vz_recv.at[k], left).wait_recv()
+    v_right.start()
+    v_left.start()
 
     place_iota = lax.broadcasted_iota(I32, (OUT_ROWS, B), 0)
     lane = lax.broadcasted_iota(I32, (1, B), 1)
@@ -244,7 +243,7 @@
     pooled_t = qz[z]
     for o in range(1, NZ):
         k = (z + o) % NZ
-        remote(qz.at[k], zr.at[k], z_send.at[o - 1], z_recv.at[k], left).wait_recv()
+        remote(qz.at[k], zr.at[k], z_send.at[0], z_recv.at[k], left).wait_recv()
         pooled_t = pooled_t + zr[k]
     pooled = pooled_t.T
 
@@ -288,12 +287,10 @@
         grads[0, slot] = high
         grads[1, slot] = low
 
-    parts = [(zh + 1 + z // 2) % ZH, (zh + 2 + 2 * (z // 2)) % ZH, zh]
-
     def row_grads(half, i):
         rows = [
-            jnp.concatenate([et[k // 8][k % 8, half * (OWN // 256) + t * 2 + block] for k in range(CHIPS)], axis=1)
-            for t, block in ((parts[i], 0), (parts[i], 1))
+            jnp.concatenate([et[k // 8][k % 8, half * (OWN // 256) + i * 2 + block] for k in range(CHIPS)], axis=1)
+            for block in range(2)
         ]
         right_side = jnp.concatenate([grads[k].reshape(CHIPS * B, D) for k in range(2)], axis=1)
         both = jnp.dot(jnp.concatenate(rows, axis=0), right_side, preferred_element_type=F32)
@@ -307,17 +304,20 @@
         total = row_grads(c, i)
         l_out[i].wait_recv()
         outb[i] = (total + lrecv[i]).reshape(NY, HOT, D)
-        for o in (1, 7, 2, 6, 3, 5, 4, 0):
-            if i == 2 and o == 0:
-                continue
+        for o in (1, 7, 2, 6, 3, 5, 4):
             k = (y + o) % NY
-            copy = remote(outb.at[i, k], grecv.at[g], g_send.at[len(g_out)], g_recv.at[g], (parts[i] * NY + k, s))
+            copy = remote(outb.at[i, k], grecv.at[g], g_send.at[i * NY + o], g_recv.at[g], (i * NY + k, s))
             copy.start()
             g_out.append(copy)
-    grecv[g] = outb[2, y]
+
+        @pl.when(i != zh)
+        def _():
+            remote(outb.at[i, y], grecv.at[g], g_send.at[i * NY], g_recv.at[g], (i * NY + y, s)).start()
+
+    grecv[g] = outb[zh, y]
     for o in range(1, GROUPS):
         k = (g + o) % GROUPS
-        remote(grecv.at[k], grecv.at[k], g_send.at[o - 1], g_recv.at[k], left).wait_recv()
+        remote(grecv.at[k], grecv.at[k], g_send.at[0], g_recv.at[k], left).wait_recv()
     high, low = split_bf16(grecv[...].reshape(OWN, D))
     both = jnp.dot(
         jnp.concatenate([place_hot[i] for i in range(OWN // B)], axis=1),
@@ -329,8 +329,14 @@
     hot_out.wait_send()
     for copy in (*idx_out, *vz_out, *rs_out.values(), v_right, v_left, far_out, *far_on):
         copy.wait_send()
-    for copy in (*z_out, *pg_out, *l_out, *g_out):
+    for copy in (*pg_out, *l_out, *g_out):
         copy.wait_send()
+    for o in range(1, NZ):
+        k = (z + o) % NZ
+        remote(qz.at[k], zr.at[z], z_send.at[k], z_recv.at[z], at(x * NZ + k)).wait_send()
+    for o in range(1, ZH):
+        t = (zh + o) % ZH
+        remote(outb.at[t, y], grecv.at[g], g_send.at[t * NY], g_recv.at[g], (t * NY + y, s)).wait_send()
 
 
 def keep(*refs):
@@ -382,8 +388,8 @@
             pltpu.VMEM((GROUPS, HOT, D), F32),
             pltpu.VMEM((OWN // B, OUT_ROWS, B), BF16),
             dma((8,)), dma((2,)), dma((CHIPS - 1,)), dma((CHIPS,)), dma((NZ - 1,)), dma((NZ,)), dma((NZ,)), dma((NZ,)), dma((2,)), dma((2,)),
-            dma((6,)), dma((6,)), dma((NZ - 1,)), dma((NZ,)), dma((CHIPS - 1,)), dma((CHIPS,)),
-            dma((ZH,)), dma((ZH,)), dma((GROUPS - 1,)), dma((GROUPS,)),
+            dma((6,)), dma((6,)), dma((NZ,)), dma((NZ,)), dma((CHIPS - 1,)), dma((CHIPS,)),
+            dma((ZH,)), dma((ZH,)), dma((GROUPS,)), dma((GROUPS,)),
         ],
         compiler_params=pltpu.CompilerParams(
             collective_id=0, has_side_effects=True, vmem_limit_bytes=38 * 1024 * 1024

time: 87.4 us -> 89.1 us (1.019)
  Pallas kernels: 86.6 us -> 87.7 us
    pallas_call x1, Pallas kernels: 85.8 us -> 86.8 us  [on_device(): pl.pallas_call(kernel, out_shape=shapes, in_specs=[hbm] * 7, out_specs=(v...]
where the time goes in v5:
time: 89.1 us; the launch traced here: 88.3 us
  Pallas kernels  87.7 us (98%)
    pallas_call x1, Pallas kernels, on_device(): pl.pallas_call(kernel, out_shape=shapes, in_specs=[hbm] * 7, out_specs=(v...  86.8 us

profile of v5, /device:TPU:1, one launch (start us, length us, event | category | flops | bytes accessed | tf_op | source)
XLA Modules:
  0.0 88.3 jit_solution(6230677674993408341)
XLA Ops:
  0.6 86.8 %shard_map.94 = (bf16[128,1024]{1,0:T(8,128)(2,1)S(1)}, f32[128,128]{1,0:T(8,128)S(1)}, f32[328,128]{1,0:T(8,128)S(1)}) custom-call(bf16[128,128]{1,0:T(8,128)(2,1)} %bottom_hbm.1, s32[4,128]{1,0:T(4,128)} %bitcast.6, f32[1,1024]{1,0:T(1,128)} %pairs_hbm.1, s32[24,768]{1,0:T(8,128)} %starts_ref.1, f32[24,328,128]{2,1,0:T(8,128)} %bitcast.5, ...), custom_call_target="tpu_custom_call" | custom-call | tf_op jit(solution)/shard_map/pallas_call | solution.py:359
  87.5 0.8 shard_map.95

commit v6 on v5

--- a/solution.py
+++ b/solution.py
@@ -215,6 +215,12 @@
 
     lax.fori_loop(0, 4, pool_step, 0)
 
+    for o in range(1, NZ):
+        k = (z + o) % NZ
+        remote(vs.at[x, k], vs.at[x, k], vz_send.at[o - 1], vz_recv.at[k], left).wait_recv()
+    v_right.start()
+    v_left.start()
+
     for q in range(2):
         a, b = (2, 4) if q == 0 else (3, 5)
         rs_out[a].wait_recv()
@@ -225,12 +231,6 @@
             @pl.when(z != k)
             def _():
                 remote(qz.at[k], zr.at[z], z_send.at[k], z_recv.at[z], at(x * NZ + k)).start()
-
-    for o in range(1, NZ):
-        k = (z + o) % NZ
-        remote(vs.at[x, k], vs.at[x, k], vz_send.at[o - 1], vz_recv.at[k], left).wait_recv()
-    v_right.start()
-    v_left.start()
 
     place_iota = lax.broadcasted_iota(I32, (OUT_ROWS, B), 0)
     lane = lax.broadcasted_iota(I32, (1, B), 1)
@@ -287,9 +287,11 @@
         grads[0, slot] = high
         grads[1, slot] = low
 
+    parts = [(zh + 1 + z // 2) % ZH, (zh + 2 + 2 * (z // 2)) % ZH, zh]
+
     def row_grads(half, i):
         rows = [
-            jnp.concatenate([et[k // 8][k % 8, half * (OWN // 256) + i * 2 + block] for k in range(CHIPS)], axis=1)
+            jnp.concatenate([et[k // 8][k % 8, half * (OWN // 256) + parts[i] * 2 + block] for k in range(CHIPS)], axis=1)
             for block in range(2)
         ]
         right_side = jnp.concatenate([grads[k].reshape(CHIPS * B, D) for k in range(2)], axis=1)
@@ -304,17 +306,14 @@
         total = row_grads(c, i)
         l_out[i].wait_recv()
         outb[i] = (total + lrecv[i]).reshape(NY, HOT, D)
-        for o in (1, 7, 2, 6, 3, 5, 4):
+        for o in (4, 3, 5, 2, 6, 1, 7, 0):
+            if i == 2 and o == 0:
+                continue
             k = (y + o) % NY
-            copy = remote(outb.at[i, k], grecv.at[g], g_send.at[i * NY + o], g_recv.at[g], (i * NY + k, s))
+            copy = remote(outb.at[i, k], grecv.at[g], g_send.at[len(g_out)], g_recv.at[g], (parts[i] * NY + k, s))
             copy.start()
             g_out.append(copy)
-
-        @pl.when(i != zh)
-        def _():
-            remote(outb.at[i, y], grecv.at[g], g_send.at[i * NY], g_recv.at[g], (i * NY + y, s)).start()
-
-    grecv[g] = outb[zh, y]
+    grecv[g] = outb[2, y]
     for o in range(1, GROUPS):
         k = (g + o) % GROUPS
         remote(grecv.at[k], grecv.at[k], g_send.at[0], g_recv.at[k], left).wait_recv()
@@ -334,9 +333,6 @@
     for o in range(1, NZ):
         k = (z + o) % NZ
         remote(qz.at[k], zr.at[z], z_send.at[k], z_recv.at[z], at(x * NZ + k)).wait_send()
-    for o in range(1, ZH):
-        t = (zh + o) % ZH
-        remote(outb.at[t, y], grecv.at[g], g_send.at[t * NY], g_recv.at[g], (t * NY + y, s)).wait_send()
 
 
 def keep(*refs):

time: 89.1 us -> 90 us (1.010)
  Pallas kernels: 87.7 us -> 89.2 us
    pallas_call x1, Pallas kernels: 86.8 us -> 88.4 us  [on_device(): pl.pallas_call(kernel, out_shape=shapes, in_specs=[hbm] * 7, out_specs=(v...]
where the time goes in v6:
time: 90 us; the launch traced here: 89.8 us
  Pallas kernels  89.2 us (99%)
    pallas_call x1, Pallas kernels, on_device(): pl.pallas_call(kernel, out_shape=shapes, in_specs=[hbm] * 7, out_specs=(v...  88.4 us

profile of v6, /device:TPU:1, one launch (start us, length us, event | category | flops | bytes accessed | tf_op | source)
XLA Modules:
  0.0 89.8 jit_solution(7559899505510384399)
XLA Ops:
  0.6 88.4 %shard_map.94 = (bf16[128,1024]{1,0:T(8,128)(2,1)S(1)}, f32[128,128]{1,0:T(8,128)S(1)}, f32[328,128]{1,0:T(8,128)S(1)}) custom-call(bf16[128,128]{1,0:T(8,128)(2,1)} %bottom_hbm.1, s32[4,128]{1,0:T(4,128)} %bitcast.6, f32[1,1024]{1,0:T(1,128)} %pairs_hbm.1, s32[24,768]{1,0:T(8,128)} %starts_ref.1, f32[24,328,128]{2,1,0:T(8,128)} %bitcast.5, ...), custom_call_target="tpu_custom_call" | custom-call | tf_op jit(solution)/shard_map/pallas_call | solution.py:355
  89.0 0.8 shard_map.95

commit v7 on v6

--- a/solution.py
+++ b/solution.py
@@ -306,7 +306,7 @@
         total = row_grads(c, i)
         l_out[i].wait_recv()
         outb[i] = (total + lrecv[i]).reshape(NY, HOT, D)
-        for o in (4, 3, 5, 2, 6, 1, 7, 0):
+        for o in (1, 7, 2, 6, 3, 5, 4, 0):
             if i == 2 and o == 0:
                 continue
             k = (y + o) % NY

time: 90 us -> 87.2 us (0.969)
  Pallas kernels: 89.2 us -> 86.5 us
    pallas_call x1, Pallas kernels: 88.4 us -> 85.7 us  [on_device(): pl.pallas_call(kernel, out_shape=shapes, in_specs=[hbm] * 7, out_specs=(v...]
where the time goes in v7:
time: 87.2 us; the launch traced here: 87.1 us
  Pallas kernels  86.5 us (99%)
    pallas_call x1, Pallas kernels, on_device(): pl.pallas_call(kernel, out_shape=shapes, in_specs=[hbm] * 7, out_specs=(v...  85.7 us

profile of v7, /device:TPU:1, one launch (start us, length us, event | category | flops | bytes accessed | tf_op | source)
XLA Modules:
  0.0 87.1 jit_solution(17910623721400807392)
XLA Ops:
  0.6 85.7 %shard_map.94 = (bf16[128,1024]{1,0:T(8,128)(2,1)S(1)}, f32[128,128]{1,0:T(8,128)S(1)}, f32[328,128]{1,0:T(8,128)S(1)}) custom-call(bf16[128,128]{1,0:T(8,128)(2,1)} %bottom_hbm.1, s32[4,128]{1,0:T(4,128)} %bitcast.6, f32[1,1024]{1,0:T(1,128)} %pairs_hbm.1, s32[24,768]{1,0:T(8,128)} %starts_ref.1, f32[24,328,128]{2,1,0:T(8,128)} %bitcast.5, ...), custom_call_target="tpu_custom_call" | custom-call | tf_op jit(solution)/shard_map/pallas_call | solution.py:355
  86.3 0.8 shard_map.95

commit v8 on v7

--- a/solution.py
+++ b/solution.py
@@ -306,7 +306,7 @@
         total = row_grads(c, i)
         l_out[i].wait_recv()
         outb[i] = (total + lrecv[i]).reshape(NY, HOT, D)
-        for o in (1, 7, 2, 6, 3, 5, 4, 0):
+        for o in (0, 1, 7, 2, 6, 3, 5, 4):
             if i == 2 and o == 0:
                 continue
             k = (y + o) % NY

time: 87.2 us -> 88.4 us (1.014)
  Pallas kernels: 86.5 us -> 87.6 us
    pallas_call x1, Pallas kernels: 85.7 us -> 86.8 us  [on_device(): pl.pallas_call(kernel, out_shape=shapes, in_specs=[hbm] * 7, out_specs=(v...]
where the time goes in v8:
time: 88.4 us; the launch traced here: 88.3 us
  Pallas kernels  87.6 us (99%)
    pallas_call x1, Pallas kernels, on_device(): pl.pallas_call(kernel, out_shape=shapes, in_specs=[hbm] * 7, out_specs=(v...  86.8 us

profile of v8, /device:TPU:1, one launch (start us, length us, event | category | flops | bytes accessed | tf_op | source)
XLA Modules:
  0.0 88.3 jit_solution(10562635003387044362)
XLA Ops:
  0.6 86.8 %shard_map.94 = (bf16[128,1024]{1,0:T(8,128)(2,1)S(1)}, f32[128,128]{1,0:T(8,128)S(1)}, f32[328,128]{1,0:T(8,128)S(1)}) custom-call(bf16[128,128]{1,0:T(8,128)(2,1)} %bottom_hbm.1, s32[4,128]{1,0:T(4,128)} %bitcast.6, f32[1,1024]{1,0:T(1,128)} %pairs_hbm.1, s32[24,768]{1,0:T(8,128)} %starts_ref.1, f32[24,328,128]{2,1,0:T(8,128)} %bitcast.5, ...), custom_call_target="tpu_custom_call" | custom-call | tf_op jit(solution)/shard_map/pallas_call | solution.py:355
  87.5 0.8 shard_map.95
